TPU v7x, 128 devices: a whole 4x4x4 slice. The times are simulated.
128 devices in a mesh: front: 4 (over y), row: 4 (over z_lo, core), col: 8 (over x, z_hi).
Axes of the slice: x: 4, y: 4, z: 4 (z_hi: 2, z_lo: 2; z = z_hi * 2 + z_lo), core: 2. Of those that a mesh axis runs over, the one named last changes fastest.
Arguments:
- pivot_block: bfloat16 [4, 1024, 1024], P('front'), may hold values from -6 to 6
- border: bfloat16 [4, 8192, 1024], P('front', 'row'), may hold values from -6 to 6
- contrib: bfloat16 [4, 8192, 8192], P('front', 'row', 'col'), may hold values from -6 to 6
- inverses: bfloat16 [4, 4, 256, 256], P('front'), may hold values from -0.0625 to 0.0625
- row_tiles: int32 [4, 64], replicated, may hold values from 0 to 79, as said below
- col_tiles: int32 [4, 64], replicated, may hold values from 0 to 79, as said below
- owner: int32 [80], replicated, may hold values from 0 to 79, as said below
- schur_init: bfloat16 [10240, 10240], P(('front', 'row'), 'col'), may hold values from -6 to 6
- block: bfloat16 [10240, 512], P('col'), may hold values from -0.0625 to 0.0625
Outputs:
- schur: float32 [10240, 10240], P(('front', 'row'), 'col')
- product: float32 [10240, 512], P(('front', 'row', 'col'))
Inputs may be any that keep to these rules, and one draw needn't show every extreme that they name: owner is a permutation of 0 .. 79. For each front the 64 entries are distinct. With s = owner[row_tiles[f, i]], each front has exactly 4 entries in each group s // 5; among the 16 entries of one aligned block of a front at most 2 fall in one group, and that many in some block of every draw. For each front the 64 entries are distinct. With s = owner[col_tiles[f, j]], each front has exactly 8 entries in each group s // 10; among the 8 entries of one aligned block of a front at most 2 fall in one group, and that many in some block of every draw.
All inputs are finite; a program needn't handle non-finite values.
Results may differ from a plain program's by a relative error of at most 0.008.
Values may be sent and summed in bfloat16 or wider, within the bound.
A program may use at most 128 MiB of HBM per device.

v0:
```python
import jax
import jax.numpy as jnp
from jax import lax
from jax.sharding import PartitionSpec as P

TILE = 128


def in_blocks(x, dim, length):
    before, after = (x.shape[:dim], x.shape[dim + 1 :])
    return jnp.moveaxis(x.reshape(*before, length, -1, *after), dim, 0)


def sent_and_summed(x, axis, dim):
    tiles = in_blocks(x, dim, lax.axis_size(axis))
    arrived = lax.all_to_all(tiles, axis, split_axis=0, concat_axis=0, tiled=True)
    return arrived.sum(axis=0)


def eliminate(pivot, rows, inverse_set):
    panels = inverse_set.shape[0]
    width = inverse_set.shape[1]
    pivot_now = pivot.astype(jnp.float32)
    rows_now = rows.astype(jnp.float32)
    leaves = []
    for panel_index in range(panels):
        start = panel_index * width
        left = pivot_now[:, start : start + width].astype(jnp.bfloat16)
        below = jnp.arange(pivot.shape[0])[:, None] >= start + width
        lower = jnp.where(
            below, jnp.dot(left, inverse_set[panel_index], preferred_element_type=jnp.float32), 0.0
        ).astype(jnp.bfloat16)
        side = jnp.dot(
            rows_now[:, start : start + width].astype(jnp.bfloat16),
            inverse_set[panel_index],
            preferred_element_type=jnp.float32,
        ).astype(jnp.bfloat16)
        pivot_now = pivot_now - lax.dot_general(
            lower, lower, (((1,), (1,)), ((), ())), preferred_element_type=jnp.float32
        )
        rows_now = rows_now - lax.dot_general(
            side, lower, (((1,), (1,)), ((), ())), preferred_element_type=jnp.float32
        )
        leaves.append(side)
    return jnp.concatenate(leaves, axis=1)


def route_tables(slots, per_group):
    group = slots // per_group
    within = slots % per_group
    count = slots.shape[-1]
    same = group[..., :, None] == group[..., None, :]
    earlier = jnp.arange(count)[None, :] < jnp.arange(count)[:, None]
    rank = jnp.sum((same & earlier).astype(jnp.int32), axis=-1)
    return (group, rank, within)


def pick_sources(group, rank, n_groups, capacity):
    count = group.shape[-1]
    match = (group[None, None, :] == jnp.arange(n_groups)[:, None, None]) & (
        rank[None, None, :] == jnp.arange(capacity)[None, :, None]
    )
    return jnp.sum(match.astype(jnp.int32) * jnp.arange(count)[None, None, :], axis=-1)


def shards(pivot_block, border, contrib, inverses, row_tiles, col_tiles, owner, schur_init, block):
    n_front = lax.axis_size("front")
    n_row = lax.axis_size("row")
    n_col = lax.axis_size("col")
    front_index = lax.axis_index("front")
    row_index = lax.axis_index("row")
    col_index = lax.axis_index("col")
    groups = n_front * n_row
    tiles_all = row_tiles.shape[1]
    slots_all = owner.shape[0]
    row_span = border.shape[1]
    col_span = contrib.shape[2]
    tile_rows = row_span // TILE
    tile_cols = col_span // TILE
    rows_per_group = slots_all // groups
    cols_per_group = slots_all // n_col
    cap_rows = 2 * tiles_all // (n_row * groups)
    cap_cols = 2 * tiles_all // (n_col * n_col)
    share = row_span // n_col
    own_rows = lax.dynamic_slice_in_dim(border[0], col_index * share, share, 0)
    leaves = eliminate(pivot_block[0], own_rows, inverses[0])
    factor = lax.all_gather(leaves, ("row", "col"), axis=0, tiled=True)
    mine = lax.dynamic_slice_in_dim(factor, row_index * row_span, row_span, 0)
    theirs = lax.dynamic_slice_in_dim(factor, col_index * col_span, col_span, 0)
    update = (
        contrib[0].astype(jnp.float32)
        - lax.dot_general(
            mine, theirs, (((1,), (1,)), ((), ())), preferred_element_type=jnp.float32
        )
    ).astype(jnp.bfloat16)
    tiles = update.reshape(tile_rows, TILE, tile_cols, TILE)
    slot_rows = owner[row_tiles].reshape(n_front, n_row, tile_rows)
    slot_cols = owner[col_tiles].reshape(n_front, n_col, tile_cols)
    group_rows, rank_rows, within_rows = route_tables(slot_rows, rows_per_group)
    group_cols, rank_cols, within_cols = route_tables(slot_cols, cols_per_group)
    send_rows = pick_sources(
        group_rows[front_index, row_index], rank_rows[front_index, row_index], groups, cap_rows
    )
    my_group = front_index * n_row + row_index
    flat_group = group_rows.reshape(groups, tile_rows)
    flat_rank = rank_rows.reshape(groups, tile_rows)
    flat_within = within_rows.reshape(groups, tile_rows)
    hit_rows = (flat_group == my_group)[:, None, :] & (
        flat_rank[:, None, :] == jnp.arange(cap_rows)[None, :, None]
    )
    place_rows = jnp.sum(
        (
            hit_rows[None]
            & (flat_within[None, :, None, :] == jnp.arange(rows_per_group)[:, None, None, None])
        ).astype(jnp.int32),
        axis=-1,
    ).astype(jnp.bfloat16)
    hit_cols = (group_cols == col_index)[:, :, None, :] & (
        rank_cols[:, :, None, :] == jnp.arange(cap_cols)[None, None, :, None]
    )
    place_cols = jnp.sum(
        (
            hit_cols[None]
            & (
                within_cols[None, :, :, None, :]
                == jnp.arange(cols_per_group)[:, None, None, None, None]
            )
        ).astype(jnp.int32),
        axis=-1,
    ).astype(jnp.bfloat16)
    place_cols = jnp.repeat(place_cols, n_row, axis=1)
    send_cols = pick_sources(
        group_cols[front_index, col_index], rank_cols[front_index, col_index], n_col, cap_cols
    )
    by_rows = jnp.take(tiles, send_rows.reshape(-1), axis=0)
    by_both = jnp.take(by_rows, send_cols.reshape(-1), axis=2)
    outgoing = by_both.reshape(groups, cap_rows, TILE, n_col, cap_cols, TILE).transpose(
        0, 3, 1, 4, 2, 5
    )
    outgoing = outgoing.reshape(groups * n_col, cap_rows, cap_cols, TILE, TILE)
    received = lax.all_to_all(
        outgoing, ("front", "row", "col"), split_axis=0, concat_axis=0, tiled=True
    )
    received = received.reshape(groups, n_col, cap_rows, cap_cols, TILE, TILE)
    gathered = jnp.einsum(
        "bgcm,gckmxy->bgkxy", place_cols, received, preferred_element_type=jnp.float32
    ).astype(jnp.bfloat16)
    summed = jnp.einsum("agk,bgkxy->abxy", place_rows, gathered, preferred_element_type=jnp.float32)
    schur = schur_init.astype(jnp.float32) + summed.transpose(0, 2, 1, 3).reshape(
        rows_per_group * TILE, cols_per_group * TILE
    )
    rounded = schur.astype(jnp.bfloat16)
    product = sent_and_summed(jnp.dot(rounded, block, preferred_element_type=jnp.float32), "col", 0)
    return (schur, product)


def solution(mesh):
    in_specs = (
        P("front", None, None),
        P("front", "row", None),
        P("front", "row", "col"),
        P("front", None, None, None),
        P(),
        P(),
        P(),
        P(("front", "row"), "col"),
        P("col", None),
    )
    out_specs = (P(("front", "row"), "col"), P(("front", "row", "col"), None))
    return jax.shard_map(shards, mesh=mesh, in_specs=in_specs, out_specs=out_specs, check_vma=False)
```

profile of v0, /device:TPU:13, one launch (start us, length us, event | category | flops | bytes accessed | tf_op | source)
XLA Modules:
  0.0 533.7 jit_solution(2947707500783428051)
XLA Ops:
  7.3 1.2 dynamic-slice_bitcast_fusion
  8.5 1.1 convolution_convert_fusion.3
  9.7 1.4 fusion.19
  11.1 0.7 convert_subtract_fusion.1
  11.8 0.4 convolution_subtract_fusion.1
  12.2 0.2 convolution_convert_fusion.2
  12.4 0.3 fusion.20
  12.8 2.7 fusion.59
  15.5 0.3 convolution_subtract_fusion
  15.9 0.9 convolution_convert_fusion.1
  16.7 2.2 fusion.22
  18.9 1.1 convolution_convert_fusion
  20.1 1.8 pad_maximum_fusion
  22.0 2.0 gather_fusion
  24.1 0.1 and.166
  24.2 0.1 div.47
  24.3 0.4 convert_reduce_fusion.2
  24.8 0.1 select_reduce_fusion
  24.9 0.1 copy.23
  25.0 0.1 reshape.422
  25.1 0.1 reshape.420
  25.3 1.9 gather_fusion.1
  27.2 0.1 ne.123
  27.5 0.7 convert_reduce_fusion.1
  28.3 0.1 select_reduce_fusion.1
  28.5 0.1 copy.22
  28.7 118.5 %all-gather.2.cloned.1.call-done = bf16[8192,1024]{0,1:T(8,128)(2,1)} async-done(((bf16[256,1024]{0,1:T(8,128)(2,1)}), bf16[8192,1024]{0,1:T(8,128)(2,1)}) %all-gather.2.cloned.1.call-update) | async-done | bytes 16777232 | tf_op jit(solution)/shard_map/all_gather | solution.py:87
  147.2 8.7 %fusion.8 = bf16[256,8,8,128]{3,1,2,0:T(8,128)(2,1)S(1)} fusion(bf16[1,2048,1024]{2,1,0:T(8,128)(2,1)} %param.11, bf16[8192,1024]{0,1:T(8,128)(2,1)} %all-gather.2.cloned.1.call-done, s32[]{:T(128)S(6)} %select_n.153, s32[]{:T(128)S(6)} %select_n.154), kind=kOutput, calls=%fused_computation.14 | convolution fusion | flops 4301258752 | bytes 14680072 | tf_op jit(solution)/shard_map/dot_general | solution.py:92
  155.9 3.1 copy.39
  159.0 7.1 %gather_fusion.2 = bf16[32,128,8,128]{3,2,1,0:T(8,128)(2,1)} fusion(bf16[16,128,8,128]{3,2,1,0:T(8,128)(2,1)} %bitcast.87, s32[1024]{0:T(1024)S(1)} %pad_clamp_fusion.1), kind=kCustom, calls=%fused_computation.2 | custom fusion | bytes 16777344 | tf_op jit(solution)/shard_map/jit(_take)/gather | solution.py:135
  166.1 7.5 %broadcast_select_fusion = bf16[32,128,8,128]{3,2,1,0:T(8,128)(2,1)} fusion(bf16[32,128,8,128]{3,2,1,0:T(8,128)(2,1)} %gather_fusion.2, pred[32]{0:T(512)(128)(4,1)S(1)} %compare_and_fusion.2), kind=kLoop, calls=%fused_computation.13 | loop fusion | flops 4194304 | bytes 16777248 | tf_op jit(solution)/shard_map/jit(_take)/select_n | solution.py:135
  173.6 8.8 %copy.26 = bf16[32,128,8,128]{3,1,0,2:T(8,128)(2,1)} copy(bf16[32,128,8,128]{3,2,1,0:T(8,128)(2,1)} %broadcast_select_fusion) | data formatting | bytes 16777216 | tf_op jit(solution)/shard_map/jit(_take)/select_n | solution.py:135
  182.4 10.4 %gather_fusion.3 = bf16[16,32,128,128]{3,2,1,0:T(8,128)(2,1)} fusion(bf16[32,128,8,128]{3,1,0,2:T(8,128)(2,1)} %copy.26, s32[1024]{0:T(1024)S(1)} %pad_clamp_fusion), kind=kCustom, calls=%fused_computation.3 | custom fusion | bytes 33554496 | tf_op jit(solution)/shard_map/jit(_take)/gather | solution.py:136
  192.8 14.1 %copy_select_fusion = bf16[16,2,128,8,2,128]{5,2,4,1,3,0:T(8,128)(2,1)} fusion(bf16[16,2,128,8,2,128]{5,2,1,0,4,3:T(8,128)(2,1)} %bitcast.86, pred[8,2]{1,0:T(8,128)(4,1)S(1)} %copy.22), kind=kLoop, calls=%fused_computation.8 | loop fusion | flops 8388608 | bytes 33554448 | tf_op jit(solution)/shard_map/jit(_take)/select_n | solution.py:136
  206.9 9.6 %all-to-all-start = ((bf16[128,2,2,128,128]{4,3,2,1,0:T(8,128)(2,1)}), bf16[128,2,2,128,128]{4,3,2,1,0:T(8,128)(2,1)}, u32[]{:S(2)}, u32[]{:S(2)}) async-start(bf16[128,2,2,128,128]{4,3,2,1,0:T(8,128)(2,1)} %bitcast.85), calls=%async_computation | async-start | bytes 33554432 | tf_op jit(solution)/shard_map/all_to_all | solution.py:141
  216.7 0.1 ne.118
  216.9 0.1 iota_compare_fusion
  217.0 0.2 convert_reduce_fusion
  217.3 0.3 convert_reduce_fusion.3
  217.5 230.2 %all-to-all-done = bf16[128,2,2,128,128]{4,3,2,1,0:T(8,128)(2,1)} async-done(((bf16[128,2,2,128,128]{4,3,2,1,0:T(8,128)(2,1)}), bf16[128,2,2,128,128]{4,3,2,1,0:T(8,128)(2,1)}, u32[]{:S(2)}, u32[]{:S(2)}) %all-to-all-start) | async-done | bytes 16777248 | tf_op jit(solution)/shard_map/all_to_all | solution.py:141
  447.7 25.6 %fusion = bf16[10,16,2,128,128]{4,0,3,2,1:T(8,128)(2,1)} fusion(bf16[10,16,8,2,1,1]{0,2,3,5,4,1:T(8,128)(2,1)S(1)} %bitcast.91, bf16[16,8,2,2,128,128]{5,4,3,2,1,0:T(8,128)(2,1)} %bitcast.19), kind=kOutput, calls=%fused_computation.5 | convolution fusion | flops 173015040 | bytes 27268096 | tf_op jit(solution)/shard_map/bgcm,gckmxy->bgkxy/dot_general | solution.py:145
  473.4 18.8 %fusion.11 = f32[5,128,10,128]{3,0,1,2:T(8,128)S(1)} fusion(bf16[10,16,2,128,128]{4,0,3,2,1:T(8,128)(2,1)} %fusion, bf16[5,16,2,1,1]{1,2,0,4,3:T(2,128)(2,1)S(1)} %convert_bitcast_fusion), kind=kOutput, calls=%fused_computation.19 | convolution fusion | flops 52428800 | bytes 13762880 | tf_op jit(solution)/shard_map/agk,bgkxy->abxy/dot_general | solution.py:148
  492.2 2.0 copy.32
  494.2 1.7 bitcast_add_fusion
  495.9 1.0 fusion.17
  496.9 0.7 copy-done.3
  497.6 28.5 %all_to_all.10 = f32[8,80,512]{2,1,0:T(8,128)S(1)} all-to-all(f32[8,80,512]{2,1,0:T(8,128)S(1)} %bitcast.90), channel_id=1, replica_groups=mesh['front'=4,'row'=4,'col'=8] {'col'}, dimensions={0} | all-to-all | bytes 2621440 | tf_op jit(solution)/shard_map/all_to_all | solution.py:16
  526.1 0.8 reduce_sum.69
  (67 shorter events, 1.1 us)
Async XLA Ops:
  7.2 488.7 %copy-start = (bf16[1280,512]{1,0:T(8,128)(2,1)S(1)}, bf16[1280,512]{1,0:T(8,128)(2,1)}, u32[]{:S(2)}) copy-start(bf16[1280,512]{1,0:T(8,128)(2,1)} %param.17) | copy-start | bytes 3932164
  7.2 3.9 copy-start.4
  7.2 140.0 %all-gather.2.cloned.1.call-start = ((), (), s32[]{:S(2)}) async-start(), calls=%async_computation.2 | async-start | bytes 17301504 | tf_op jit(solution)/shard_map/all_gather | solution.py:87
  11.1 1.1 copy-start.6
  11.8 3.7 copy-start.2
  12.4 3.4 copy-start.7
  15.5 6.4 %copy-start.8 = (s32[4,64]{1,0:T(4,128)S(1)}, s32[4,64]{1,0:T(4,128)}, u32[]{:S(2)}) copy-start(s32[4,64]{1,0:T(4,128)} %param.14) | copy-start | bytes 3076
  15.5 6.4 %copy-start.9 = (s32[4,64]{1,0:T(4,128)S(1)}, s32[4,64]{1,0:T(4,128)}, u32[]{:S(2)}) copy-start(s32[4,64]{1,0:T(4,128)} %param.13) | copy-start | bytes 3076
  15.5 6.5 %copy-start.1 = (s32[80]{0:T(128)S(1)}, s32[80]{0:T(128)}, u32[]{:S(2)}) copy-start(s32[80]{0:T(128)} %param.15) | copy-start | bytes 964
  206.9 240.8 %all-to-all-start = ((bf16[128,2,2,128,128]{4,3,2,1,0:T(8,128)(2,1)}), bf16[128,2,2,128,128]{4,3,2,1,0:T(8,128)(2,1)}, u32[]{:S(2)}, u32[]{:S(2)}) async-start(bf16[128,2,2,128,128]{4,3,2,1,0:T(8,128)(2,1)} %bitcast.85), calls=%async_computation | async-start | bytes 33554432 | tf_op jit(solution)/shard_map/all_to_all | solution.py:141
  492.2 2.0 copy-start.5
  495.9 1.7 copy-start.3
Sparse Core Ops, SparseCore 0:
  22.0 125.1 all-gather.1
where the time goes:
time: 540 us; the launch traced here: 534 us
  waiting for transfers between devices  349 us (65%)
  matrix products  65.6 us (12%)
  local copies, waits for them, and re-layouts  38.8 us (7%)
  blocking collectives  28.5 us (5%)
  other arithmetic  28 us (5%)
  between operations  14.5 us (3%)
  starting transfers between devices  9.69 us (2%)
    all_to_all x1, waiting for transfers between devices, shards(): lax.all_to_all(outgoing, ('front', 'row', 'col'), split_axis=0, concat_ax...  230 us
    all_gather x1, waiting for transfers between devices, shards(): factor = lax.all_gather(leaves, ('row', 'col'), axis=0, tiled=True)  118 us
    all_to_all x1, blocking collectives, sent_and_summed(): lax.all_to_all(tiles, axis, split_axis=0, concat_axis=0, tiled=True)  28.5 us
    dot_general x1, matrix products, shards(): jnp.einsum('bgcm,gckmxy->bgkxy', place_cols, received, preferred_element_...  25.6 us
    dot_general x1, matrix products, shards(): jnp.einsum('agk,bgkxy->abxy', place_rows, gathered, preferred_element_typ...  18.8 us
    select_n x2, other arithmetic, shards(): by_both = jnp.take(by_rows, send_cols.reshape(-1), axis=2)  14.1 us
  transfers between devices with their start and end apart: 2, of which 2 were waited for; matrix products, arithmetic and copies ran while one was open for 1% of the time, Pallas kernels for 0%

commit v1 on v0

v1 whole, which is shorter than its diff:
```python
import functools

import jax
import jax.numpy as jnp
from jax import lax
from jax.experimental import pallas as pl
from jax.experimental.pallas import tpu as pltpu
from jax.sharding import PartitionSpec as P

TILE = 128
MESH = pl.DeviceIdType.MESH
F32 = jnp.float32
BF16 = jnp.bfloat16


def nt(a, b):
    return lax.dot_general(a, b, (((1,), (1,)), ((), ())), preferred_element_type=F32)


def split_levels(src_c, src_r, dst_c, dst_r, squarings):
    n = src_c.shape[0]
    at_c = lax.broadcasted_iota(jnp.int32, (n, n), 0).astype(F32)
    at_r = lax.broadcasted_iota(jnp.int32, (n, n), 1).astype(F32)
    color_c = jnp.zeros((n, 1), F32)
    color_r = jnp.zeros((1, n), F32)

    def partners(node_c, node_r):
        same = jnp.where((node_c == node_r) & (color_c == color_r), 1.0, 0.0)
        rank_c = jnp.sum(jnp.where(at_r < at_c, same, 0.0), axis=1, keepdims=True)
        rank_r = jnp.sum(jnp.where(at_c < at_r, same, 0.0), axis=0, keepdims=True)
        pair = (jnp.floor(rank_c * 0.5) == jnp.floor(rank_r * 0.5)) & (at_c != at_r)
        return jnp.where(pair, same, 0.0)

    for count in squarings:
        by_src = partners(src_c, src_r)
        by_dst = partners(dst_c, dst_r)
        reach = jnp.dot(by_src.astype(BF16), by_dst.astype(BF16), preferred_element_type=F32)
        reach = jnp.where(at_c == at_r, 1.0, reach)
        for _ in range(count):
            half = reach.astype(BF16)
            reach = jnp.where(jnp.dot(half, half, preferred_element_type=F32) > 0.5, 1.0, 0.0)
        far = float(n)
        label_c = jnp.min(jnp.where(reach > 0.5, at_r, far), axis=1, keepdims=True)
        label_r = jnp.min(jnp.where(reach > 0.5, at_c, far), axis=0, keepdims=True)
        other_c = jnp.sum(by_src * label_r, axis=1, keepdims=True)
        other_r = jnp.sum(by_src * label_c, axis=0, keepdims=True)
        color_c = color_c * 2.0 + jnp.where(label_c > other_c, 1.0, 0.0)
        color_r = color_r * 2.0 + jnp.where(label_r > other_r, 1.0, 0.0)
    return color_c


def div(x, by):
    return jnp.floor((x + 0.5) * (1.0 / by))


def routing(rows_c, rows_r, cols_c, cols_r, owner_r, owner_c, front, row, col):
    n = rows_c.shape[0]
    per = n // 4
    slots = owner_r.shape[1]
    lane = lax.broadcasted_iota(jnp.int32, (n, slots), 1)
    sub = lax.broadcasted_iota(jnp.int32, (slots, n), 0)
    own_r = owner_r.astype(F32)
    own_c = owner_c.astype(F32)

    def slot_c(ids):
        return jnp.sum(jnp.where(ids == lane, own_r, 0.0), axis=1, keepdims=True)

    def slot_r(ids):
        return jnp.sum(jnp.where(ids == sub, own_c, 0.0), axis=0, keepdims=True)

    e_c = lax.broadcasted_iota(jnp.int32, (n, 1), 0).astype(F32)
    e_r = lax.broadcasted_iota(jnp.int32, (1, n), 1).astype(F32)
    f_c, f_r = div(e_c, per), div(e_r, per)
    i_c = e_c - f_c * per
    rs_c, rs_r, cs_c, cs_r = slot_c(rows_c), slot_r(rows_r), slot_c(cols_c), slot_r(cols_r)
    g_c, g_r, h_c, h_r = div(rs_c, 5), div(rs_r, 5), div(cs_c, 10), div(cs_r, 10)
    a_c, b_c = rs_c - g_c * 5, cs_c - h_c * 10
    mr = split_levels(div(e_c, 4), div(e_r, 4), f_c * 16 + g_c, f_r * 16 + g_r, (5, 4))
    mc = split_levels(div(e_c, 8), div(e_r, 8), f_c * 8 + h_c, f_r * 8 + h_r, (5, 4, 3))
    front, row, col = front.astype(F32), row.astype(F32), col.astype(F32)
    mine = f_c == front
    q = lax.broadcasted_iota(jnp.int32, (n, TILE), 1).astype(F32)

    def table(mask, value):
        return jnp.sum(jnp.where(mask, value, 0.0), axis=0, keepdims=True)

    in_row = i_c - div(i_c, 16) * 16
    chunk = div(in_row, 4)
    t0 = table(mine & (div(i_c, 16) == row) & (mr * 4 + chunk == q), in_row)
    block = div(i_c, 8)
    t1 = table(mine & (block == col) & (mc == q), i_c - block * 8)
    t2 = table(mine & (mr == row) & (g_c == q), div(i_c, 4))
    t3 = table(mine & (mc == col) & (h_c == q), block)
    t4 = table((g_c == front * 4 + row) & (f_c * 5 + a_c == q), mr + 1.0)
    t5 = table((h_c == col) & (f_c * 10 + b_c == q), mc + 1.0)
    zero = jnp.zeros_like(t0)
    return jnp.concatenate([t0, t1, t2, t3, t4, t5, zero, zero], axis=0).astype(jnp.int32)


def routing_kernel(rows_c, rows_r, cols_c, cols_r, owner_r, owner_c, out):
    out[...] = routing(
        rows_c[...], rows_r[...], cols_c[...], cols_r[...], owner_r[...], owner_c[...],
        lax.axis_index("front"), lax.axis_index("row"), lax.axis_index("col"),
    )


def route_tables(row_tiles, col_tiles, owner):
    n, slots = row_tiles.size, owner.size
    return pl.pallas_call(
        routing_kernel,
        out_shape=jax.ShapeDtypeStruct((8, TILE), jnp.int32),
        name="route_tables",
    )(
        row_tiles.reshape(n, 1), row_tiles.reshape(1, n), col_tiles.reshape(n, 1), col_tiles.reshape(1, n),
        owner.reshape(1, slots), owner.reshape(slots, 1),
    )


def position():
    front, row, col = lax.axis_index("front"), lax.axis_index("row"), lax.axis_index("col")
    return front, row // 2, row % 2, col // 2, col % 2


def device(front, z, core, x):
    return (front, (z % 2) * 2 + core, x * 2 + z // 2)


def eliminate_rows(block, lower, inverse_set):
    parts = []
    for k in range(4):
        now = block[:, k * 256 : (k + 1) * 256].astype(F32)
        for j in range(k):
            now = now - nt(parts[j], lower[k * 256 : (k + 1) * 256, j * 256 : (j + 1) * 256])
        parts.append(
            jnp.dot(now.astype(BF16), inverse_set[k], preferred_element_type=F32).astype(BF16)
        )
    return parts


def update_kernel(
    tab, pivot, border, contrib, inverse_set, out,
    rows_v, theirs, theirs_p, contrib_v, lower, out_v, lsem, osem, ssem, rsem,
):
    front, z_lo, core, x, z_hi = position()
    z = z_hi * 2 + z_lo
    up, down = (z + 1) % 4, (z + 3) % 4
    on_source_chip = z_lo == x // 2
    is_source = on_source_chip & (core == x % 2)
    sibling = device(front, z, 1 - core, x)
    barrier = pltpu.get_barrier_semaphore()
    for peer in (sibling, *(device(front, zz, k, x) for zz in (up, down) for k in (0, 1))):
        pl.semaphore_signal(barrier, inc=1, device_id=peer, device_id_type=MESH)
    load_lower = pltpu.make_async_copy(pivot.at[0], lower, lsem.at[0])
    load_rows = pltpu.make_async_copy(border, rows_v, lsem.at[1])
    load_contrib = [
        pltpu.make_async_copy(
            contrib.at[:, :, j * TILE : (j + 1) * TILE], contrib_v.at[j], lsem.at[2 + j]
        )
        for j in range(8)
    ]
    load_lower.start()
    load_rows.start()
    for copy in load_contrib:
        copy.start()
    pl.semaphore_wait(barrier, 5)

    def push(src, quarter, sem, peer):
        return pltpu.make_async_remote_copy(
            src_ref=src, dst_ref=theirs.at[pl.ds(2 * quarter, 2)], send_sem=ssem.at[sem], recv_sem=rsem.at[quarter],
            device_id=peer, device_id_type=MESH,
        )

    def quarter_of(half, q):
        return border.at[pl.ds(half * 8 + q * 2, 2)]

    def source_sends():
        sends = []
        for q in (0, 1):
            sends.append(push(quarter_of(up // 2, q), q, q, device(front, up, q, x)))
            sends.append(push(quarter_of(down // 2, 2 + q), 2 + q, 2 + q, device(front, down, q, x)))
        for q in range(4):
            sends.append(push(quarter_of(z_hi, q), q, 4 + q, sibling))
        return sends

    def own_quarters():
        return [pltpu.make_async_copy(quarter_of(z_hi, q), theirs.at[pl.ds(2 * q, 2)], lsem.at[11 + q]) for q in range(4)]

    @pl.when(is_source)
    def _():
        for copy in source_sends():
            copy.start()
        for copy in own_quarters():
            copy.start()

    load_lower.wait()
    for k in range(3):
        low = (k + 1) * 256
        now = lower[low:, k * 256 : (k + 1) * 256].astype(F32)
        for j in range(k):
            now = now - nt(
                lower[low:, j * 256 : (j + 1) * 256], lower[k * 256 : low, j * 256 : (j + 1) * 256]
            )
        lower[low:, k * 256 : (k + 1) * 256] = jnp.dot(
            now.astype(BF16), inverse_set[0, k], preferred_element_type=F32
        ).astype(BF16)
    load_rows.wait()

    def own_block(i, _):
        rows = pl.ds(i * 4, 4)
        parts = eliminate_rows(rows_v[rows].reshape(512, 1024), lower, inverse_set.at[0])
        for k in range(4):
            rows_v[rows, :, k * 256 : (k + 1) * 256] = parts[k].reshape(4, TILE, 256)
        return 0

    lax.fori_loop(0, 4, own_block, 0)

    def wait_quarter(q):
        push(theirs.at[pl.ds(2 * q, 2)], q, 0, sibling).wait_recv()

    def forwards():
        return [
            push(theirs.at[pl.ds(2 * q, 2)], q, i, sibling) for i, q in enumerate((core, 2 + core))
        ]

    @pl.when(is_source)
    def _():
        for copy in own_quarters():
            copy.wait()

    @pl.when(jnp.logical_not(on_source_chip))
    def _():
        first, second = forwards()
        wait_quarter(core)
        first.start()
        wait_quarter(2 + core)
        second.start()
        wait_quarter(1 - core)
        wait_quarter(3 - core)

    @pl.when(on_source_chip & jnp.logical_not(is_source))
    def _():
        for q in range(4):
            wait_quarter(q)

    @pl.when(is_source)
    def _():
        for copy in source_sends():
            copy.wait_send()

    @pl.when(jnp.logical_not(on_source_chip))
    def _():
        for copy in forwards():
            copy.wait_send()

    def their_block(i, _):
        rows = pl.ds(i * 4, 4)
        parts = eliminate_rows(theirs[rows].reshape(512, 1024), lower, inverse_set.at[0])
        for k in range(4):
            theirs[rows, :, k * 256 : (k + 1) * 256] = parts[k].reshape(4, TILE, 256)
        return 0

    lax.fori_loop(0, 2, their_block, 0)
    for m in range(8):
        theirs_p[m] = theirs[tab[1, m]]
    for copy in load_contrib:
        copy.wait()

    def packed(mr):
        return pltpu.make_async_copy(out_v.at[mr], out.at[mr], osem.at[mr])

    for mr in range(4):
        left = jnp.concatenate([rows_v[tab[0, mr * 4 + k]] for k in range(4)], axis=0)

        def two_cols(n, _):
            product = nt(left, theirs_p[pl.ds(n * 2, 2)].reshape(256, 1024))
            for t in range(2):
                for k in range(4):
                    tile = contrib_v[tab[1, 2 * n + t], tab[0, mr * 4 + k]].astype(F32)
                    part = product[k * TILE : (k + 1) * TILE, t * TILE : (t + 1) * TILE]
                    out_v[mr, 2 * n + t, k] = (tile - part).astype(BF16)
            return 0

        lax.fori_loop(0, 4, two_cols, 0)
        packed(mr).start()
    for mr in range(4):
        packed(mr).wait()


def packed_update(tables, pivot, border, contrib, inverse_set):
    vmem = pl.BlockSpec(memory_space=pltpu.VMEM)
    hbm = pl.BlockSpec(memory_space=pl.ANY)
    return pl.pallas_call(
        update_kernel,
        out_shape=jax.ShapeDtypeStruct((4, 8, 4, TILE, TILE), BF16),
        in_specs=[pl.BlockSpec(memory_space=pltpu.SMEM), hbm, hbm, hbm, vmem],
        out_specs=hbm,
        scratch_shapes=[
            pltpu.VMEM((16, TILE, 1024), BF16),
            pltpu.VMEM((8, TILE, 1024), BF16),
            pltpu.VMEM((8, TILE, 1024), BF16),
            pltpu.VMEM((8, 16, TILE, TILE), BF16),
            pltpu.VMEM((1024, 1024), BF16),
            pltpu.VMEM((4, 8, 4, TILE, TILE), BF16),
            pltpu.SemaphoreType.DMA((15,)),
            pltpu.SemaphoreType.DMA((4,)),
            pltpu.SemaphoreType.DMA((8,)),
            pltpu.SemaphoreType.DMA((4,)),
        ],
        compiler_params=pltpu.CompilerParams(
            collective_id=0, has_side_effects=True, vmem_limit_bytes=60 << 20
        ),
        name="packed_update",
    )(tables, pivot, border.reshape(16, TILE, 1024), contrib.reshape(16, TILE, 1024), inverse_set)


def reorder_kernel(tab, arrived, out):
    for h in range(8):
        out[0, h] = arrived[0, tab[3, h], 0]


def reorder(tables, arrived):
    return pl.pallas_call(
        reorder_kernel,
        out_shape=jax.ShapeDtypeStruct((16, 8, TILE, TILE), BF16),
        grid_spec=pltpu.PrefetchScalarGridSpec(
            num_scalar_prefetch=1,
            grid=(16,),
            in_specs=[
                pl.BlockSpec(
                    (1, 8, 1, TILE, TILE), lambda g, tab: (tab[2, g] // 4, 0, tab[2, g] % 4, 0, 0)
                )
            ],
            out_specs=pl.BlockSpec((1, 8, TILE, TILE), lambda g, tab: (g, 0, 0, 0)),
        ),
        name="reorder",
    )(tables, arrived.reshape(4, 8, 4, TILE, TILE))


def assemble_kernel(tab, t0, t1, t2, t3, init, vectors, schur, partial):
    a = pl.program_id(0)
    tiles = (t0, t1, t2, t3)
    for b in range(10):
        cols = slice(b * TILE, (b + 1) * TILE)
        total = init[:, cols].astype(F32)
        for f in range(4):
            m = tab[5, f * 10 + b]
            there = (m > 0) & (tab[4, f * 5 + a] > 0)
            tile = tiles[f][0, 0, jnp.maximum(m - 1, 0)].astype(F32)
            total = total + jnp.where(there, tile, 0.0)
        schur[:, cols] = total
    partial[...] = jnp.dot(
        schur[...].astype(BF16), vectors[...], preferred_element_type=F32
    ).astype(partial.dtype)


def assemble(tables, arrived, init, vectors):
    def pick(f):
        return pl.BlockSpec(
            (1, 1, 8, TILE, TILE), lambda a, tab: (f, jnp.maximum(tab[4, f * 5 + a] - 1, 0), 0, 0, 0)
        )

    arrived = arrived.reshape(4, 4, 8, TILE, TILE)
    rows, cols = init.shape
    wide = vectors.shape[1]
    return pl.pallas_call(
        assemble_kernel,
        out_shape=(
            jax.ShapeDtypeStruct((rows, cols), F32),
            jax.ShapeDtypeStruct((rows, wide), BF16),
        ),
        grid_spec=pltpu.PrefetchScalarGridSpec(
            num_scalar_prefetch=1,
            grid=(rows // TILE,),
            in_specs=[
                *(pick(f) for f in range(4)),
                pl.BlockSpec((TILE, cols), lambda a, tab: (a, 0)),
                pl.BlockSpec((cols, wide), lambda a, tab: (0, 0)),
            ],
            out_specs=(
                pl.BlockSpec((TILE, cols), lambda a, tab: (a, 0)),
                pl.BlockSpec((TILE, wide), lambda a, tab: (a, 0)),
            ),
        ),
        name="assemble",
    )(tables, arrived, arrived, arrived, arrived, init, vectors)


def shards(pivot_block, border, contrib, inverses, row_tiles, col_tiles, owner, schur_init, block):
    tables = route_tables(row_tiles, col_tiles, owner)
    packed = packed_update(tables, pivot_block, border, contrib, inverses)
    spread = lax.all_to_all(
        packed.reshape(32, 4, TILE, TILE), ("row", "col"), split_axis=0, concat_axis=0, tiled=True
    )
    ordered = reorder(tables, spread)
    arrived = lax.all_to_all(
        ordered.reshape(128, TILE, TILE), ("front", "row", "col"), split_axis=0, concat_axis=0, tiled=True
    )
    schur, partial = assemble(tables, arrived, schur_init, block)
    parts = lax.all_to_all(
        partial.reshape(8, 80, 512), "col", split_axis=0, concat_axis=0, tiled=True
    )
    product = parts.astype(F32).sum(axis=0)
    return schur, product


def solution(mesh):
    in_specs = (
        P("front", None, None),
        P("front", "row", None),
        P("front", "row", "col"),
        P("front", None, None, None),
        P(),
        P(),
        P(),
        P(("front", "row"), "col"),
        P("col", None),
    )
    out_specs = (P(("front", "row"), "col"), P(("front", "row", "col"), None))
    return jax.shard_map(shards, mesh=mesh, in_specs=in_specs, out_specs=out_specs, check_vma=False)
```

time: 540 us -> 203 us (0.38)
  the two profiles are of different devices: /device:TPU:13 before, /device:TPU:0 now
where the time goes in v1:
time: 203 us; the launch traced here: 202 us
  blocking collectives  138 us (68%)
  Pallas kernels  55.9 us (28%)
  local copies, waits for them, and re-layouts  6.95 us (3%)
    all_to_all x1, blocking collectives, shards(): lax.all_to_all(ordered.reshape(128, TILE, TILE), ('front', 'row', 'col'),...  60.2 us
    all_to_all x1, blocking collectives, shards(): lax.all_to_all(packed.reshape(32, 4, TILE, TILE), ('row', 'col'), split_a...  59.5 us
    pallas_call x1, Pallas kernels, packed_update(): pl.pallas_call(update_kernel, out_shape=jax.ShapeDtypeStruct((4, 8, 4, TI...  29.3 us
    all_to_all x1, blocking collectives, shards(): lax.all_to_all(partial.reshape(8, 80, 512), 'col', split_axis=0, concat_a...  18 us
    pallas_call x1, Pallas kernels, reorder(): pl.pallas_call(reorder_kernel, out_shape=jax.ShapeDtypeStruct((16, 8, TIL...  10.9 us
    pallas_call x1, Pallas kernels, assemble(): pl.pallas_call(assemble_kernel, out_shape=(jax.ShapeDtypeStruct((rows, co...  7.98 us
    pallas_call x1, Pallas kernels, route_tables(): pl.pallas_call(routing_kernel, out_shape=jax.ShapeDtypeStruct((8, TILE),...  7.71 us

profile of v1, /device:TPU:0, one launch (start us, length us, event | category | flops | bytes accessed | tf_op | source)
XLA Modules:
  0.0 202.0 jit_solution(5763190934124882182)
XLA Ops:
  0.6 1.3 reshape.44.rows_r
  2.0 1.5 reshape.56.rows_c
  3.4 1.3 reshape.46.cols_r
  4.7 1.5 reshape.57.cols_c
  6.2 1.4 copy.14.owner_c
  7.6 7.7 %route_tables.1.tab = s32[8,128]{1,0:T(8,128)} custom-call(s32[256,1]{1,0:T(8,128)} %reshape.56.rows_c, s32[1,256]{1,0:T(1,128)} %reshape.44.rows_r, s32[256,1]{1,0:T(8,128)} %reshape.57.cols_c, s32[1,256]{1,0:T(1,128)} %reshape.46.cols_r, s32[1,80]{1,0:T(1,128)} %bitcast.20, s32[80,1]{1,0:T(8,128)} %copy.14.owner_c), custom_call_target="tpu_custom_call" | custom-call | tf_op jit(solution)/shard_map/route_tables/pallas_call | solution.py:109
  15.3 29.3 %packed_update.1 = bf16[4,8,4,128,128]{4,3,2,1,0:T(8,128)(2,1)} custom-call(s32[8,128]{1,0:T(8,128)} %route_tables.1.tab, bf16[1,1024,1024]{2,1,0:T(8,128)(2,1)} %pivot.1, bf16[16,128,1024]{2,1,0:T(8,128)(2,1)} %bitcast.16, bf16[16,128,1024]{2,1,0:T(8,128)(2,1)} %bitcast.17, bf16[1,4,256,256]{3,2,1,0:T(8,128)(2,1)} %inverse_set.1), custom_call_target="tpu_custom_call" | custom-call | tf_op jit(solution)/shard_map/packed_update/pallas_call | solution.py:292
  44.6 59.5 %all_to_all.15 = bf16[32,4,128,128]{3,2,1,0:T(8,128)(2,1)} all-to-all(bf16[32,4,128,128]{3,2,1,0:T(8,128)(2,1)} %bitcast.15), channel_id=1, replica_groups=mesh['front'=4,'row'=4,'col'=8] {'row','col'}, dimensions={0} | all-to-all | bytes 8388608 | tf_op jit(solution)/shard_map/all_to_all | solution.py:391
  104.1 10.9 %reorder.1 = bf16[16,8,128,128]{3,2,1,0:T(8,128)(2,1)} custom-call(s32[8,128]{1,0:T(8,128)} %route_tables.1.tab, bf16[4,8,4,128,128]{4,3,2,1,0:T(8,128)(2,1)} %bitcast.13), custom_call_target="tpu_custom_call" | custom-call | tf_op jit(solution)/shard_map/reorder/pallas_call | solution.py:322
  115.0 60.2 %all_to_all.16 = bf16[128,128,128]{2,1,0:T(8,128)(2,1)} all-to-all(bf16[128,128,128]{2,1,0:T(8,128)(2,1)} %bitcast.14), channel_id=1, replica_groups=mesh['front'=4,'row'=4,'col'=8] {'front','row','col'}, dimensions={0} | all-to-all | bytes 8388608 | tf_op jit(solution)/shard_map/all_to_all | solution.py:395
  175.2 8.0 %assemble.1 = (f32[640,1280]{1,0:T(8,128)}, bf16[640,512]{1,0:T(8,128)(2,1)}) custom-call(s32[8,128]{1,0:T(8,128)} %route_tables.1.tab, bf16[4,4,8,128,128]{4,3,2,1,0:T(8,128)(2,1)} %bitcast.9, bf16[4,4,8,128,128]{4,3,2,1,0:T(8,128)(2,1)} %bitcast.10, bf16[4,4,8,128,128]{4,3,2,1,0:T(8,128)(2,1)} %bitcast.11, bf16[4,4,8,128,128]{4,3,2,1,0:T(8,128)(2,1)} %bitcast.12, ...), custom_call_target="tpu_custom_call" | custom-call | tf_op jit(solution)/shard_map/assemble/pallas_call | solution.py:365
  183.2 18.0 %all_to_all.17 = bf16[8,80,512]{2,1,0:T(8,128)(2,1)S(1)} all-to-all(bf16[8,80,512]{2,1,0:T(8,128)(2,1)} %bitcast.18), channel_id=1, replica_groups=mesh['front'=4,'row'=4,'col'=8] {'col'}, dimensions={0} | all-to-all | bytes 1310720 | tf_op jit(solution)/shard_map/all_to_all | solution.py:399
  201.2 0.8 convert_reduce_fusion

commit v2 on v1

--- a/solution.py
+++ b/solution.py
@@ -89,31 +89,32 @@
     t0 = table(mine & (div(i_c, 16) == row) & (mr * 4 + chunk == q), in_row)
     block = div(i_c, 8)
     t1 = table(mine & (block == col) & (mc == q), i_c - block * 8)
-    t2 = table(mine & (mr == row) & (g_c == q), div(i_c, 4))
+    at_row = mine & (mr == row) & (g_c == q)
+    t2 = table(at_row, div(i_c, 16) * 8)
     t3 = table(mine & (mc == col) & (h_c == q), block)
+    t6 = table(at_row, chunk)
     t4 = table((g_c == front * 4 + row) & (f_c * 5 + a_c == q), mr + 1.0)
     t5 = table((h_c == col) & (f_c * 10 + b_c == q), mc + 1.0)
     zero = jnp.zeros_like(t0)
-    return jnp.concatenate([t0, t1, t2, t3, t4, t5, zero, zero], axis=0).astype(jnp.int32)
-
-
-def routing_kernel(rows_c, rows_r, cols_c, cols_r, owner_r, owner_c, out):
-    out[...] = routing(
-        rows_c[...], rows_r[...], cols_c[...], cols_r[...], owner_r[...], owner_c[...],
-        lax.axis_index("front"), lax.axis_index("row"), lax.axis_index("col"),
+    return jnp.concatenate([t0, t1, t2, t3, t4, t5, t6, zero], axis=0).astype(jnp.int32)
+
+
+def both_ways(ids):
+    fronts, per = ids.shape
+    n = fronts * per
+    spread = jnp.where(
+        lax.broadcasted_iota(jnp.int32, (per, n), 0) == lax.broadcasted_iota(jnp.int32, (per, n), 1) % per, 1.0, 0.0
     )
-
-
-def route_tables(row_tiles, col_tiles, owner):
-    n, slots = row_tiles.size, owner.size
-    return pl.pallas_call(
-        routing_kernel,
-        out_shape=jax.ShapeDtypeStruct((8, TILE), jnp.int32),
-        name="route_tables",
-    )(
-        row_tiles.reshape(n, 1), row_tiles.reshape(1, n), col_tiles.reshape(n, 1), col_tiles.reshape(1, n),
-        owner.reshape(1, slots), owner.reshape(slots, 1),
-    )
+    wide = jnp.dot(ids.astype(F32).astype(BF16), spread.astype(BF16), preferred_element_type=F32)
+    here = lax.broadcasted_iota(jnp.int32, (fronts, n), 0) == lax.broadcasted_iota(jnp.int32, (fronts, n), 1) // per
+    flat = jnp.sum(jnp.where(here, wide, 0.0), axis=0, keepdims=True)
+    return turned(flat).astype(jnp.int32), flat.astype(jnp.int32)
+
+
+def turned(flat):
+    n = flat.shape[1]
+    eye = lax.broadcasted_iota(jnp.int32, (n, n), 0) == lax.broadcasted_iota(jnp.int32, (n, n), 1)
+    return jnp.sum(jnp.where(eye, flat, 0.0), axis=1, keepdims=True)
 
 
 def position():
@@ -137,9 +138,9 @@
     return parts
 
 
-def update_kernel(
-    tab, pivot, border, contrib, inverse_set, out,
-    rows_v, theirs, theirs_p, contrib_v, lower, out_v, lsem, osem, ssem, rsem,
+def eliminate_kernel(
+    row_tiles, col_tiles, owner, pivot, border, inverse_set, tab, own_out, theirs_out,
+    rows_v, theirs, lower, lsem, osem, ssem, rsem,
 ):
     front, z_lo, core, x, z_hi = position()
     z = z_hi * 2 + z_lo
@@ -152,22 +153,14 @@
         pl.semaphore_signal(barrier, inc=1, device_id=peer, device_id_type=MESH)
     load_lower = pltpu.make_async_copy(pivot.at[0], lower, lsem.at[0])
     load_rows = pltpu.make_async_copy(border, rows_v, lsem.at[1])
-    load_contrib = [
-        pltpu.make_async_copy(
-            contrib.at[:, :, j * TILE : (j + 1) * TILE], contrib_v.at[j], lsem.at[2 + j]
-        )
-        for j in range(8)
-    ]
     load_lower.start()
     load_rows.start()
-    for copy in load_contrib:
-        copy.start()
     pl.semaphore_wait(barrier, 5)
 
     def push(src, quarter, sem, peer):
         return pltpu.make_async_remote_copy(
-            src_ref=src, dst_ref=theirs.at[pl.ds(2 * quarter, 2)], send_sem=ssem.at[sem], recv_sem=rsem.at[quarter],
-            device_id=peer, device_id_type=MESH,
+            src_ref=src, dst_ref=theirs.at[pl.ds(2 * quarter, 2)], send_sem=ssem.at[sem],
+            recv_sem=rsem.at[quarter], device_id=peer, device_id_type=MESH,
         )
 
     def quarter_of(half, q):
@@ -183,7 +176,10 @@
         return sends
 
     def own_quarters():
-        return [pltpu.make_async_copy(quarter_of(z_hi, q), theirs.at[pl.ds(2 * q, 2)], lsem.at[11 + q]) for q in range(4)]
+        return [
+            pltpu.make_async_copy(quarter_of(z_hi, q), theirs.at[pl.ds(2 * q, 2)], lsem.at[2 + q])
+            for q in range(4)
+        ]
 
     @pl.when(is_source)
     def _():
@@ -205,14 +201,24 @@
         ).astype(BF16)
     load_rows.wait()
 
-    def own_block(i, _):
-        rows = pl.ds(i * 4, 4)
-        parts = eliminate_rows(rows_v[rows].reshape(512, 1024), lower, inverse_set.at[0])
-        for k in range(4):
-            rows_v[rows, :, k * 256 : (k + 1) * 256] = parts[k].reshape(4, TILE, 256)
-        return 0
-
-    lax.fori_loop(0, 4, own_block, 0)
+    def block_of(buffer, target, base):
+        def step(i, _):
+            rows = pl.ds(i * 4, 4)
+            parts = eliminate_rows(buffer[rows].reshape(512, 1024), lower, inverse_set.at[0])
+            for k in range(4):
+                buffer[rows, :, k * 256 : (k + 1) * 256] = parts[k].reshape(4, TILE, 256)
+            pltpu.make_async_copy(buffer.at[rows], target.at[rows], osem.at[base + i]).start()
+            return 0
+
+        return step
+
+    lax.fori_loop(0, 4, block_of(rows_v, own_out, 0), 0)
+    rows_c, rows_r = both_ways(row_tiles[...])
+    cols_c, cols_r = both_ways(col_tiles[...])
+    tab[...] = routing(
+        rows_c, rows_r, cols_c, cols_r, owner[...], turned(owner[...].astype(F32)),
+        front, lax.axis_index("row"), lax.axis_index("col"),
+    )
 
     def wait_quarter(q):
         push(theirs.at[pl.ds(2 * q, 2)], q, 0, sibling).wait_recv()
@@ -252,88 +258,217 @@
         for copy in forwards():
             copy.wait_send()
 
-    def their_block(i, _):
+    lax.fori_loop(0, 2, block_of(theirs, theirs_out, 4), 0)
+    for i in range(4):
         rows = pl.ds(i * 4, 4)
-        parts = eliminate_rows(theirs[rows].reshape(512, 1024), lower, inverse_set.at[0])
-        for k in range(4):
-            theirs[rows, :, k * 256 : (k + 1) * 256] = parts[k].reshape(4, TILE, 256)
-        return 0
-
-    lax.fori_loop(0, 2, their_block, 0)
-    for m in range(8):
-        theirs_p[m] = theirs[tab[1, m]]
-    for copy in load_contrib:
-        copy.wait()
-
-    def packed(mr):
-        return pltpu.make_async_copy(out_v.at[mr], out.at[mr], osem.at[mr])
-
-    for mr in range(4):
-        left = jnp.concatenate([rows_v[tab[0, mr * 4 + k]] for k in range(4)], axis=0)
-
-        def two_cols(n, _):
-            product = nt(left, theirs_p[pl.ds(n * 2, 2)].reshape(256, 1024))
-            for t in range(2):
-                for k in range(4):
-                    tile = contrib_v[tab[1, 2 * n + t], tab[0, mr * 4 + k]].astype(F32)
-                    part = product[k * TILE : (k + 1) * TILE, t * TILE : (t + 1) * TILE]
-                    out_v[mr, 2 * n + t, k] = (tile - part).astype(BF16)
-            return 0
-
-        lax.fori_loop(0, 4, two_cols, 0)
-        packed(mr).start()
-    for mr in range(4):
-        packed(mr).wait()
-
-
-def packed_update(tables, pivot, border, contrib, inverse_set):
+        pltpu.make_async_copy(rows_v.at[rows], own_out.at[rows], osem.at[i]).wait()
+    for i in range(2):
+        rows = pl.ds(i * 4, 4)
+        pltpu.make_async_copy(theirs.at[rows], theirs_out.at[rows], osem.at[4 + i]).wait()
+
+
+def eliminate(row_tiles, col_tiles, owner, pivot, border, inverse_set):
     vmem = pl.BlockSpec(memory_space=pltpu.VMEM)
     hbm = pl.BlockSpec(memory_space=pl.ANY)
     return pl.pallas_call(
-        update_kernel,
-        out_shape=jax.ShapeDtypeStruct((4, 8, 4, TILE, TILE), BF16),
-        in_specs=[pl.BlockSpec(memory_space=pltpu.SMEM), hbm, hbm, hbm, vmem],
+        eliminate_kernel,
+        out_shape=(
+            jax.ShapeDtypeStruct((8, TILE), jnp.int32),
+            jax.ShapeDtypeStruct((16, TILE, 1024), BF16),
+            jax.ShapeDtypeStruct((8, TILE, 1024), BF16),
+        ),
+        in_specs=[vmem, vmem, vmem, hbm, hbm, vmem],
+        out_specs=(vmem, hbm, hbm),
+        scratch_shapes=[
+            pltpu.VMEM((16, TILE, 1024), BF16),
+            pltpu.VMEM((8, TILE, 1024), BF16),
+            pltpu.VMEM((1024, 1024), BF16),
+            pltpu.SemaphoreType.DMA((6,)),
+            pltpu.SemaphoreType.DMA((6,)),
+            pltpu.SemaphoreType.DMA((8,)),
+            pltpu.SemaphoreType.DMA((4,)),
+        ],
+        compiler_params=pltpu.CompilerParams(
+            collective_id=0, has_side_effects=True, vmem_limit_bytes=60 << 20
+        ),
+        name="eliminate",
+    )(
+        row_tiles, col_tiles, owner.reshape(1, owner.size), pivot,
+        border.reshape(16, TILE, 1024), inverse_set,
+    )
+
+
+PARTS = 2
+PART = TILE // PARTS
+
+
+def peer_of(front, z, core, x, u):
+    dk, dx, dz, dy = u % 2, (u // 2) % 4, (u // 8) % 4, u // 32
+    f2, z2, k2, x2 = (front + dy) % 4, (z + dz) % 4, (core + dk) % 2, (x + dx) % 4
+    row, col = (z2 % 2) * 2 + k2, x2 * 2 + z2 // 2
+    return f2, row, col
+
+
+def exchange_kernel(
+    tab, own, theirs, contrib, out,
+    own_v, theirs_v, theirs_p, contrib_v, left, packed, ordered, lsem, s1, r1, s2, r2, *spread,
+):
+    front, z_lo, core, x, z_hi = position()
+    z = z_hi * 2 + z_lo
+    row, col = lax.axis_index("row"), lax.axis_index("col")
+    here = row * 8 + col
+    everywhere = front * 32 + here
+    barrier = pltpu.get_barrier_semaphore()
+
+    def greet(u, _):
+        pl.semaphore_signal(barrier, inc=1, device_id=peer_of(front, z, core, x, u), device_id_type=MESH)
+        return 0
+
+    lax.fori_loop(1, 128, greet, 0)
+    load_theirs = pltpu.make_async_copy(theirs, theirs_v, lsem.at[0])
+    load_own = pltpu.make_async_copy(own, own_v, lsem.at[1])
+    load_contrib = [
+        pltpu.make_async_copy(
+            contrib.at[:, :, j * TILE : (j + 1) * TILE], contrib_v.at[j], lsem.at[2 + j]
+        )
+        for j in range(8)
+    ]
+    load_theirs.start()
+    load_own.start()
+    for copy in load_contrib:
+        copy.start()
+    load_theirs.wait()
+    for m in range(8):
+        theirs_p[m] = theirs_v[tab[1, m]]
+    load_own.wait()
+    for copy in load_contrib:
+        copy.wait()
+
+    def update(s):
+        for q in range(16):
+            left[q] = own_v[tab[0, q], s * PART : (s + 1) * PART]
+
+        def two_cols(n, _):
+            product = nt(
+                left[...].reshape(16 * PART, 1024), theirs_p[pl.ds(n * 2, 2)].reshape(256, 1024)
+            )
+            for t in range(2):
+                for q in range(16):
+                    tile = contrib_v[tab[1, 2 * n + t], tab[0, q], s * PART : (s + 1) * PART].astype(F32)
+                    part = product[q * PART : (q + 1) * PART, t * TILE : (t + 1) * TILE]
+                    packed[s, (q // 4) * 8 + 2 * n + t, q % 4] = (tile - part).astype(BF16)
+            return 0
+
+        lax.fori_loop(0, 4, two_cols, 0)
+
+    def first_send(s):
+        def send(t, _):
+            _, row2, col2 = peer_of(front, z, core, x, (t * 11) % 32)
+            pltpu.make_async_remote_copy(
+                src_ref=packed.at[s, row2 * 8 + col2], dst_ref=spread[s].at[here],
+                send_sem=s1.at[s], recv_sem=r1.at[s],
+                device_id=(front, row2, col2), device_id_type=MESH,
+            ).start()
+            return 0
+
+        lax.fori_loop(1, 32, send, 0)
+        spread[s][here] = packed[s, here]
+
+    def first_all(s):
+        return pltpu.make_async_remote_copy(
+            src_ref=packed.at[s, pl.ds(0, 31)], dst_ref=spread[s].at[pl.ds(0, 31)],
+            send_sem=s1.at[s], recv_sem=r1.at[s],
+            device_id=(front, row, col), device_id_type=MESH,
+        )
+
+    GROUP = 8
+
+    def second_peer(t):
+        return peer_of(front, z, core, x, (t * 37) % 128)
+
+    def second_copy(s, t):
+        f2, row2, col2 = second_peer(t)
+        return pltpu.make_async_remote_copy(
+            src_ref=ordered.at[s, t], dst_ref=out.at[s, everywhere],
+            send_sem=s2.at[s], recv_sem=r2.at[s],
+            device_id=(f2, row2, col2), device_id_type=MESH,
+        )
+
+    def second_self(s):
+        return pltpu.make_async_copy(ordered.at[s, 0], out.at[s, everywhere], lsem.at[10 + s])
+
+    def second_send(s):
+        def fill(t):
+            f2, row2, col2 = second_peer(t)
+            g = f2 * 4 + row2
+            ordered[s, t] = spread[s][tab[2, g] + tab[3, col2], tab[6, g]]
+
+        for t in range(GROUP):
+            fill(t)
+        second_self(s).start()
+
+        def step(i, _):
+            for t in range(GROUP):
+                fill(i * GROUP + t)
+            for t in range(GROUP):
+                at = (i - 1) * GROUP + t
+
+                @pl.when(at > 0)
+                def _():
+                    second_copy(s, at).start()
+
+            return 0
+
+        lax.fori_loop(1, 128 // GROUP, step, 0)
+        for t in range(GROUP):
+            second_copy(s, 128 - GROUP + t).start()
+
+    def second_all(s):
+        return pltpu.make_async_remote_copy(
+            src_ref=ordered.at[s, pl.ds(0, 127)], dst_ref=out.at[s, pl.ds(0, 127)],
+            send_sem=s2.at[s], recv_sem=r2.at[s],
+            device_id=(front, row, col), device_id_type=MESH,
+        )
+
+    for s in range(PARTS):
+        update(s)
+        if s == 0:
+            pl.semaphore_wait(barrier, 127)
+        first_send(s)
+    for s in range(PARTS):
+        first_all(s).wait_recv()
+        second_send(s)
+    for s in range(PARTS):
+        first_all(s).wait_send()
+        second_self(s).wait()
+        second_all(s).wait_recv()
+        second_all(s).wait_send()
+
+
+def exchanged_update(tables, own, theirs, contrib):
+    hbm = pl.BlockSpec(memory_space=pl.ANY)
+    return pl.pallas_call(
+        exchange_kernel,
+        out_shape=jax.ShapeDtypeStruct((PARTS, 128, PART, TILE), BF16),
+        in_specs=[pl.BlockSpec(memory_space=pltpu.SMEM), hbm, hbm, hbm],
         out_specs=hbm,
         scratch_shapes=[
             pltpu.VMEM((16, TILE, 1024), BF16),
             pltpu.VMEM((8, TILE, 1024), BF16),
             pltpu.VMEM((8, TILE, 1024), BF16),
             pltpu.VMEM((8, 16, TILE, TILE), BF16),
-            pltpu.VMEM((1024, 1024), BF16),
-            pltpu.VMEM((4, 8, 4, TILE, TILE), BF16),
-            pltpu.SemaphoreType.DMA((15,)),
-            pltpu.SemaphoreType.DMA((4,)),
-            pltpu.SemaphoreType.DMA((8,)),
-            pltpu.SemaphoreType.DMA((4,)),
+            pltpu.VMEM((16, PART, 1024), BF16),
+            pltpu.VMEM((PARTS, 32, 4, PART, TILE), BF16),
+            pltpu.VMEM((PARTS, 128, PART, TILE), BF16),
+            pltpu.SemaphoreType.DMA((10 + PARTS,)),
+            *[pltpu.SemaphoreType.DMA((PARTS,))] * 4,
+            *[pltpu.VMEM((32, 4, PART, TILE), BF16)] * PARTS,
         ],
         compiler_params=pltpu.CompilerParams(
-            collective_id=0, has_side_effects=True, vmem_limit_bytes=60 << 20
+            collective_id=1, has_side_effects=True, vmem_limit_bytes=60 << 20
         ),
-        name="packed_update",
-    )(tables, pivot, border.reshape(16, TILE, 1024), contrib.reshape(16, TILE, 1024), inverse_set)
-
-
-def reorder_kernel(tab, arrived, out):
-    for h in range(8):
-        out[0, h] = arrived[0, tab[3, h], 0]
-
-
-def reorder(tables, arrived):
-    return pl.pallas_call(
-        reorder_kernel,
-        out_shape=jax.ShapeDtypeStruct((16, 8, TILE, TILE), BF16),
-        grid_spec=pltpu.PrefetchScalarGridSpec(
-            num_scalar_prefetch=1,
-            grid=(16,),
-            in_specs=[
-                pl.BlockSpec(
-                    (1, 8, 1, TILE, TILE), lambda g, tab: (tab[2, g] // 4, 0, tab[2, g] % 4, 0, 0)
-                )
-            ],
-            out_specs=pl.BlockSpec((1, 8, TILE, TILE), lambda g, tab: (g, 0, 0, 0)),
-        ),
-        name="reorder",
-    )(tables, arrived.reshape(4, 8, 4, TILE, TILE))
+        name="exchanged_update",
+    )(tables, own, theirs, contrib.reshape(16, TILE, 1024))
 
 
 def assemble_kernel(tab, t0, t1, t2, t3, init, vectors, schur, partial):
@@ -341,13 +476,15 @@
     tiles = (t0, t1, t2, t3)
     for b in range(10):
         cols = slice(b * TILE, (b + 1) * TILE)
-        total = init[:, cols].astype(F32)
-        for f in range(4):
-            m = tab[5, f * 10 + b]
-            there = (m > 0) & (tab[4, f * 5 + a] > 0)
-            tile = tiles[f][0, 0, jnp.maximum(m - 1, 0)].astype(F32)
-            total = total + jnp.where(there, tile, 0.0)
-        schur[:, cols] = total
+        for s in range(PARTS):
+            rows = slice(s * PART, (s + 1) * PART)
+            total = init[rows, cols].astype(F32)
+            for f in range(4):
+                m = tab[5, f * 10 + b]
+                there = (m > 0) & (tab[4, f * 5 + a] > 0)
+                tile = tiles[f][s, 0, 0, jnp.maximum(m - 1, 0)].astype(F32)
+                total = total + jnp.where(there, tile, 0.0)
+            schur[rows, cols] = total
     partial[...] = jnp.dot(
         schur[...].astype(BF16), vectors[...], preferred_element_type=F32
     ).astype(partial.dtype)
@@ -356,10 +493,11 @@
 def assemble(tables, arrived, init, vectors):
     def pick(f):
         return pl.BlockSpec(
-            (1, 1, 8, TILE, TILE), lambda a, tab: (f, jnp.maximum(tab[4, f * 5 + a] - 1, 0), 0, 0, 0)
-        )
-
-    arrived = arrived.reshape(4, 4, 8, TILE, TILE)
+            (PARTS, 1, 1, 8, PART, TILE),
+            lambda a, tab: (0, f, jnp.maximum(tab[4, f * 5 + a] - 1, 0), 0, 0, 0),
+        )
+
+    arrived = arrived.reshape(PARTS, 4, 4, 8, PART, TILE)
     rows, cols = init.shape
     wide = vectors.shape[1]
     return pl.pallas_call(
@@ -385,22 +523,52 @@
     )(tables, arrived, arrived, arrived, arrived, init, vectors)
 
 
+def product_kernel(partial, out, arrived, ssem, rsem):
+    front, row, col = lax.axis_index("front"), lax.axis_index("row"), lax.axis_index("col")
+    barrier = pltpu.get_barrier_semaphore()
+    others = [(col + d) % 8 for d in range(1, 8)]
+    for other in others:
+        pl.semaphore_signal(barrier, inc=1, device_id=(front, row, other), device_id_type=MESH)
+    pl.semaphore_wait(barrier, 7)
+    copies = [
+        pltpu.make_async_remote_copy(
+            src_ref=partial.at[other], dst_ref=arrived.at[d], send_sem=ssem.at[d], recv_sem=rsem.at[d],
+            device_id=(front, row, other), device_id_type=MESH,
+        )
+        for d, other in enumerate(others)
+    ]
+    for copy in copies:
+        copy.start()
+    total = partial[col].astype(F32)
+    for d, copy in enumerate(copies):
+        copy.wait()
+        total = total + arrived[d].astype(F32)
+    out[...] = total
+
+
+def product_sum(partial):
+    vmem = pl.BlockSpec(memory_space=pltpu.VMEM)
+    _, rows, wide = partial.shape
+    return pl.pallas_call(
+        product_kernel,
+        out_shape=jax.ShapeDtypeStruct((rows, wide), F32),
+        in_specs=[vmem],
+        out_specs=vmem,
+        scratch_shapes=[
+            pltpu.VMEM((7, rows, wide), BF16),
+            pltpu.SemaphoreType.DMA((7,)),
+            pltpu.SemaphoreType.DMA((7,)),
+        ],
+        compiler_params=pltpu.CompilerParams(collective_id=2, has_side_effects=True),
+        name="product_sum",
+    )(partial)
+
+
 def shards(pivot_block, border, contrib, inverses, row_tiles, col_tiles, owner, schur_init, block):
-    tables = route_tables(row_tiles, col_tiles, owner)
-    packed = packed_update(tables, pivot_block, border, contrib, inverses)
-    spread = lax.all_to_all(
-        packed.reshape(32, 4, TILE, TILE), ("row", "col"), split_axis=0, concat_axis=0, tiled=True
-    )
-    ordered = reorder(tables, spread)
-    arrived = lax.all_to_all(
-        ordered.reshape(128, TILE, TILE), ("front", "row", "col"), split_axis=0, concat_axis=0, tiled=True
-    )
+    tables, own, theirs = eliminate(row_tiles, col_tiles, owner, pivot_block, border, inverses)
+    arrived = exchanged_update(tables, own, theirs, contrib)
     schur, partial = assemble(tables, arrived, schur_init, block)
-    parts = lax.all_to_all(
-        partial.reshape(8, 80, 512), "col", split_axis=0, concat_axis=0, tiled=True
-    )
-    product = parts.astype(F32).sum(axis=0)
-    return schur, product
+    return schur, product_sum(partial.reshape(8, 80, 512))
 
 
 def solution(mesh):

time: 203 us -> 181 us (0.89)
  the two profiles are of different devices: /device:TPU:0 before, /device:TPU:13 now
where the time goes in v2:
time: 181 us; the launch traced here: 179 us
  Pallas kernels  177 us (98%)
    pallas_call x1, Pallas kernels, exchanged_update(): pl.pallas_call(exchange_kernel, out_shape=jax.ShapeDtypeStruct((PARTS, 12...  121 us
    pallas_call x1, Pallas kernels, eliminate(): pl.pallas_call(eliminate_kernel, out_shape=(jax.ShapeDtypeStruct((8, TILE...  24.7 us
    pallas_call x1, Pallas kernels, product_sum(): pl.pallas_call(product_kernel, out_shape=jax.ShapeDtypeStruct((rows, wide...  23 us
    pallas_call x1, Pallas kernels, assemble(): pl.pallas_call(assemble_kernel, out_shape=(jax.ShapeDtypeStruct((rows, co...  8.08 us

profile of v2, /device:TPU:13, one launch (start us, length us, event | category | flops | bytes accessed | tf_op | source)
XLA Modules:
  0.0 178.8 jit_solution(4329017403526426095)
XLA Ops:
  0.6 24.7 %eliminate.1 = (s32[8,128]{1,0:T(8,128)}, bf16[16,128,1024]{2,1,0:T(8,128)(2,1)}, bf16[8,128,1024]{2,1,0:T(8,128)(2,1)}) custom-call(s32[4,64]{1,0:T(4,128)} %row_tiles.1, s32[4,64]{1,0:T(4,128)} %col_tiles.1, s32[1,80]{1,0:T(1,128)} %bitcast.12, bf16[1,1024,1024]{2,1,0:T(8,128)(2,1)} %pivot.1, bf16[16,128,1024]{2,1,0:T(8,128)(2,1)} %bitcast.9, ...), custom_call_target="tpu_custom_call" | custom-call | tf_op jit(solution)/shard_map/eliminate/pallas_call | solution.py:273
  25.4 120.8 %exchanged_update.1 = bf16[2,128,64,128]{3,2,1,0:T(8,128)(2,1)} custom-call(s32[8,128]{1,0:T(8,128)} %get-tuple-element.7.tab, bf16[16,128,1024]{2,1,0:T(8,128)(2,1)} %get-tuple-element.8.own, bf16[8,128,1024]{2,1,0:T(8,128)(2,1)} %get-tuple-element.9.theirs, bf16[16,128,1024]{2,1,0:T(8,128)(2,1)} %bitcast.10), custom_call_target="tpu_custom_call" | custom-call | tf_op jit(solution)/shard_map/exchanged_update/pallas_call | solution.py:450
  146.2 8.1 %assemble.1 = (f32[640,1280]{1,0:T(8,128)}, bf16[640,512]{1,0:T(8,128)(2,1)}) custom-call(s32[8,128]{1,0:T(8,128)} %get-tuple-element.7.tab, bf16[2,4,4,8,64,128]{5,4,3,2,1,0:T(8,128)(2,1)} %bitcast.5, bf16[2,4,4,8,64,128]{5,4,3,2,1,0:T(8,128)(2,1)} %bitcast.6, bf16[2,4,4,8,64,128]{5,4,3,2,1,0:T(8,128)(2,1)} %bitcast.7, ...), custom_call_target="tpu_custom_call" | custom-call | tf_op jit(solution)/shard_map/assemble/pallas_call | solution.py:503
  154.2 23.0 %product_sum.1 = f32[80,512]{1,0:T(8,128)} custom-call(bf16[8,80,512]{2,1,0:T(8,128)(2,1)} %bitcast.11), custom_call_target="tpu_custom_call" | custom-call | tf_op jit(solution)/shard_map/product_sum/pallas_call | solution.py:552
  177.3 1.6 copy.12

commit v3 on v2

--- a/solution.py
+++ b/solution.py
@@ -298,21 +298,31 @@
     )
 
 
-PARTS = 2
-PART = TILE // PARTS
+PARTS = 8
+
+
+ORDER1 = 11
+ORDER2 = 37
 
 
 def peer_of(front, z, core, x, u):
-    dk, dx, dz, dy = u % 2, (u // 2) % 4, (u // 8) % 4, u // 32
-    f2, z2, k2, x2 = (front + dy) % 4, (z + dz) % 4, (core + dk) % 2, (x + dx) % 4
-    row, col = (z2 % 2) * 2 + k2, x2 * 2 + z2 // 2
-    return f2, row, col
+    dk, dx, dz, dy = u & 1, (u >> 1) & 3, (u >> 3) & 3, u >> 5
+    f2, z2, k2, x2 = (front + dy) & 3, (z + dz) & 3, core ^ dk, (x + dx) & 3
+    return f2, ((z2 & 1) << 1) + k2, (x2 << 1) + (z2 >> 1)
+
+
+GROUP = 8
+UNIT = 16
 
 
 def exchange_kernel(
-    tab, own, theirs, contrib, out,
-    own_v, theirs_v, theirs_p, contrib_v, left, packed, ordered, lsem, s1, r1, s2, r2, *spread,
+    tab, own, theirs, contrib, init, vectors, schur, product,
+    own_v, theirs_v, theirs_p, contrib_v, left, packed, ordered, init_v, vectors_v, schur_v, rounded, partial, sums,
+    lsem, s1, r1, s2, r2, osem, s3, r3, *buffers,
 ):
+    spread, landed = buffers[:PARTS], buffers[PARTS:]
+    size = TILE // PARTS
+    units = size // UNIT
     front, z_lo, core, x, z_hi = position()
     z = z_hi * 2 + z_lo
     row, col = lax.axis_index("row"), lax.axis_index("col")
@@ -329,14 +339,18 @@
     load_own = pltpu.make_async_copy(own, own_v, lsem.at[1])
     load_contrib = [
         pltpu.make_async_copy(
-            contrib.at[:, :, j * TILE : (j + 1) * TILE], contrib_v.at[j], lsem.at[2 + j]
+            contrib.at[:, :, j * TILE : (j + 1) * TILE], contrib_v.at[j], lsem.at[4 + j]
         )
         for j in range(8)
     ]
+    load_init = pltpu.make_async_copy(init, init_v, lsem.at[2])
+    load_vectors = pltpu.make_async_copy(vectors, vectors_v, lsem.at[3])
     load_theirs.start()
     load_own.start()
     for copy in load_contrib:
         copy.start()
+    load_init.start()
+    load_vectors.start()
     load_theirs.wait()
     for m in range(8):
         theirs_p[m] = theirs_v[tab[1, m]]
@@ -345,17 +359,18 @@
         copy.wait()
 
     def update(s):
+        rows = slice(s * size, (s + 1) * size)
         for q in range(16):
-            left[q] = own_v[tab[0, q], s * PART : (s + 1) * PART]
+            left[q] = own_v[tab[0, q], rows]
 
         def two_cols(n, _):
             product = nt(
-                left[...].reshape(16 * PART, 1024), theirs_p[pl.ds(n * 2, 2)].reshape(256, 1024)
+                left[...].reshape(16 * size, 1024), theirs_p[pl.ds(n * 2, 2)].reshape(256, 1024)
             )
             for t in range(2):
                 for q in range(16):
-                    tile = contrib_v[tab[1, 2 * n + t], tab[0, q], s * PART : (s + 1) * PART].astype(F32)
-                    part = product[q * PART : (q + 1) * PART, t * TILE : (t + 1) * TILE]
+                    tile = contrib_v[tab[1, 2 * n + t], tab[0, q], rows].astype(F32)
+                    part = product[q * size : (q + 1) * size, t * TILE : (t + 1) * TILE]
                     packed[s, (q // 4) * 8 + 2 * n + t, q % 4] = (tile - part).astype(BF16)
             return 0
 
@@ -363,7 +378,7 @@
 
     def first_send(s):
         def send(t, _):
-            _, row2, col2 = peer_of(front, z, core, x, (t * 11) % 32)
+            _, row2, col2 = peer_of(front, z, core, x, (t * ORDER1) & 31)
             pltpu.make_async_remote_copy(
                 src_ref=packed.at[s, row2 * 8 + col2], dst_ref=spread[s].at[here],
                 send_sem=s1.at[s], recv_sem=r1.at[s],
@@ -381,21 +396,15 @@
             device_id=(front, row, col), device_id_type=MESH,
         )
 
-    GROUP = 8
-
     def second_peer(t):
-        return peer_of(front, z, core, x, (t * 37) % 128)
+        return peer_of(front, z, core, x, (t * ORDER2) & 127)
 
     def second_copy(s, t):
-        f2, row2, col2 = second_peer(t)
         return pltpu.make_async_remote_copy(
-            src_ref=ordered.at[s, t], dst_ref=out.at[s, everywhere],
+            src_ref=ordered.at[s, t], dst_ref=landed[s].at[everywhere],
             send_sem=s2.at[s], recv_sem=r2.at[s],
-            device_id=(f2, row2, col2), device_id_type=MESH,
-        )
-
-    def second_self(s):
-        return pltpu.make_async_copy(ordered.at[s, 0], out.at[s, everywhere], lsem.at[10 + s])
+            device_id=second_peer(t), device_id_type=MESH,
+        )
 
     def second_send(s):
         def fill(t):
@@ -405,28 +414,88 @@
 
         for t in range(GROUP):
             fill(t)
-        second_self(s).start()
+        landed[s][everywhere] = ordered[s, 0]
+        for t in range(1, GROUP):
+            second_copy(s, t).start()
 
         def step(i, _):
             for t in range(GROUP):
                 fill(i * GROUP + t)
             for t in range(GROUP):
-                at = (i - 1) * GROUP + t
-
-                @pl.when(at > 0)
-                def _():
-                    second_copy(s, at).start()
-
+                second_copy(s, i * GROUP + t).start()
             return 0
 
         lax.fori_loop(1, 128 // GROUP, step, 0)
-        for t in range(GROUP):
-            second_copy(s, 128 - GROUP + t).start()
 
     def second_all(s):
         return pltpu.make_async_remote_copy(
-            src_ref=ordered.at[s, pl.ds(0, 127)], dst_ref=out.at[s, pl.ds(0, 127)],
+            src_ref=ordered.at[s, pl.ds(0, 127)], dst_ref=landed[s].at[pl.ds(0, 127)],
             send_sem=s2.at[s], recv_sem=r2.at[s],
+            device_id=(front, row, col), device_id_type=MESH,
+        )
+
+    def strip(a, s):
+        return pl.ds(a * TILE + s * size, size)
+
+    def write(a, s):
+        return pltpu.make_async_copy(schur_v.at[strip(a, s)], schur.at[strip(a, s)], osem.at[s, a])
+
+    def assemble(s):
+        def row_of_tiles(a, _):
+            rows = pl.ds(pl.multiple_of(a * TILE + s * size, size), size)
+            for b in range(10):
+                cols = slice(b * TILE, (b + 1) * TILE)
+                total = init_v[rows, cols].astype(F32)
+                for f in range(4):
+                    m, k = tab[4, f * 5 + a], tab[5, f * 10 + b]
+                    at = f * 32 + jnp.maximum(m - 1, 0) * 8 + jnp.maximum(k - 1, 0)
+                    total = total + jnp.where((m > 0) & (k > 0), landed[s][at].astype(F32), 0.0)
+                schur_v[rows, cols] = total
+                rounded[pl.ds(pl.multiple_of(a * size, size), size), cols] = total.astype(BF16)
+            return 0
+
+        lax.fori_loop(0, 5, row_of_tiles, 0)
+        for a in range(5):
+            write(a, s).start()
+        partial[s] = (
+            jnp.dot(rounded[...], vectors_v[...], preferred_element_type=F32)
+            .astype(BF16)
+            .reshape(5, units, UNIT, partial.shape[-1])
+        )
+
+    def product_copies(s):
+        copies = []
+        for a in range(5):
+            for j in range(units):
+                u = (a * TILE + s * size) // UNIT + j
+                copies.append(
+                    (
+                        u // 5,
+                        u % 5,
+                        partial.at[s, a, j],
+                        pltpu.make_async_remote_copy(
+                            src_ref=partial.at[s, a, j], dst_ref=sums.at[col, u % 5],
+                            send_sem=s3, recv_sem=r3,
+                            device_id=(front, row, u // 5), device_id_type=MESH,
+                        ),
+                    )
+                )
+        return copies
+
+    def product_send(s):
+        for to, at, value, copy in product_copies(s):
+
+            @pl.when(col != to)
+            def _():
+                copy.start()
+
+            @pl.when(col == to)
+            def _():
+                sums[to, at] = value[...]
+
+    def product_all():
+        return pltpu.make_async_remote_copy(
+            src_ref=sums.at[pl.ds(0, 7)], dst_ref=sums.at[pl.ds(0, 7)], send_sem=s3, recv_sem=r3,
             device_id=(front, row, col), device_id_type=MESH,
         )
 
@@ -438,137 +507,71 @@
     for s in range(PARTS):
         first_all(s).wait_recv()
         second_send(s)
+    load_init.wait()
+    load_vectors.wait()
+    for s in range(PARTS):
+        second_all(s).wait_recv()
+        assemble(s)
+        product_send(s)
     for s in range(PARTS):
         first_all(s).wait_send()
-        second_self(s).wait()
-        second_all(s).wait_recv()
         second_all(s).wait_send()
-
-
-def exchanged_update(tables, own, theirs, contrib):
+    product_all().wait_recv()
+    total = sums[0].astype(F32)
+    for c in range(1, 8):
+        total = total + sums[c].astype(F32)
+    product[...] = total.reshape(product.shape)
+    product_all().wait_send()
+    for s in range(PARTS):
+        for a in range(5):
+            write(a, s).wait()
+
+
+def exchanged_update(tables, own, theirs, contrib, init, vectors):
     hbm = pl.BlockSpec(memory_space=pl.ANY)
+    size = TILE // PARTS
+    rows, cols = init.shape
+    wide = vectors.shape[1]
     return pl.pallas_call(
         exchange_kernel,
-        out_shape=jax.ShapeDtypeStruct((PARTS, 128, PART, TILE), BF16),
-        in_specs=[pl.BlockSpec(memory_space=pltpu.SMEM), hbm, hbm, hbm],
-        out_specs=hbm,
+        out_shape=(
+            jax.ShapeDtypeStruct((rows, cols), F32),
+            jax.ShapeDtypeStruct((rows // 8, wide), F32),
+        ),
+        in_specs=[pl.BlockSpec(memory_space=pltpu.SMEM), hbm, hbm, hbm, hbm, hbm],
+        out_specs=(hbm, pl.BlockSpec(memory_space=pltpu.VMEM)),
         scratch_shapes=[
             pltpu.VMEM((16, TILE, 1024), BF16),
             pltpu.VMEM((8, TILE, 1024), BF16),
             pltpu.VMEM((8, TILE, 1024), BF16),
             pltpu.VMEM((8, 16, TILE, TILE), BF16),
-            pltpu.VMEM((16, PART, 1024), BF16),
-            pltpu.VMEM((PARTS, 32, 4, PART, TILE), BF16),
-            pltpu.VMEM((PARTS, 128, PART, TILE), BF16),
-            pltpu.SemaphoreType.DMA((10 + PARTS,)),
+            pltpu.VMEM((16, size, 1024), BF16),
+            pltpu.VMEM((PARTS, 32, 4, size, TILE), BF16),
+            pltpu.VMEM((PARTS, 128, size, TILE), BF16),
+            pltpu.VMEM((rows, cols), BF16),
+            pltpu.VMEM((cols, wide), BF16),
+            pltpu.VMEM((rows, cols), F32),
+            pltpu.VMEM((5 * size, cols), BF16),
+            pltpu.VMEM((PARTS, 5, size // UNIT, UNIT, wide), BF16),
+            pltpu.VMEM((8, 5, UNIT, wide), BF16),
+            pltpu.SemaphoreType.DMA((12,)),
             *[pltpu.SemaphoreType.DMA((PARTS,))] * 4,
-            *[pltpu.VMEM((32, 4, PART, TILE), BF16)] * PARTS,
+            pltpu.SemaphoreType.DMA((PARTS, 5)),
+            pltpu.SemaphoreType.DMA,
+            pltpu.SemaphoreType.DMA,
+            *[pltpu.VMEM((32, 4, size, TILE), BF16)] * PARTS,
+            *[pltpu.VMEM((128, size, TILE), BF16)] * PARTS,
         ],
         compiler_params=pltpu.CompilerParams(
             collective_id=1, has_side_effects=True, vmem_limit_bytes=60 << 20
         ),
         name="exchanged_update",
-    )(tables, own, theirs, contrib.reshape(16, TILE, 1024))
-
-
-def assemble_kernel(tab, t0, t1, t2, t3, init, vectors, schur, partial):
-    a = pl.program_id(0)
-    tiles = (t0, t1, t2, t3)
-    for b in range(10):
-        cols = slice(b * TILE, (b + 1) * TILE)
-        for s in range(PARTS):
-            rows = slice(s * PART, (s + 1) * PART)
-            total = init[rows, cols].astype(F32)
-            for f in range(4):
-                m = tab[5, f * 10 + b]
-                there = (m > 0) & (tab[4, f * 5 + a] > 0)
-                tile = tiles[f][s, 0, 0, jnp.maximum(m - 1, 0)].astype(F32)
-                total = total + jnp.where(there, tile, 0.0)
-            schur[rows, cols] = total
-    partial[...] = jnp.dot(
-        schur[...].astype(BF16), vectors[...], preferred_element_type=F32
-    ).astype(partial.dtype)
-
-
-def assemble(tables, arrived, init, vectors):
-    def pick(f):
-        return pl.BlockSpec(
-            (PARTS, 1, 1, 8, PART, TILE),
-            lambda a, tab: (0, f, jnp.maximum(tab[4, f * 5 + a] - 1, 0), 0, 0, 0),
-        )
-
-    arrived = arrived.reshape(PARTS, 4, 4, 8, PART, TILE)
-    rows, cols = init.shape
-    wide = vectors.shape[1]
-    return pl.pallas_call(
-        assemble_kernel,
-        out_shape=(
-            jax.ShapeDtypeStruct((rows, cols), F32),
-            jax.ShapeDtypeStruct((rows, wide), BF16),
-        ),
-        grid_spec=pltpu.PrefetchScalarGridSpec(
-            num_scalar_prefetch=1,
-            grid=(rows // TILE,),
-            in_specs=[
-                *(pick(f) for f in range(4)),
-                pl.BlockSpec((TILE, cols), lambda a, tab: (a, 0)),
-                pl.BlockSpec((cols, wide), lambda a, tab: (0, 0)),
-            ],
-            out_specs=(
-                pl.BlockSpec((TILE, cols), lambda a, tab: (a, 0)),
-                pl.BlockSpec((TILE, wide), lambda a, tab: (a, 0)),
-            ),
-        ),
-        name="assemble",
-    )(tables, arrived, arrived, arrived, arrived, init, vectors)
-
-
-def product_kernel(partial, out, arrived, ssem, rsem):
-    front, row, col = lax.axis_index("front"), lax.axis_index("row"), lax.axis_index("col")
-    barrier = pltpu.get_barrier_semaphore()
-    others = [(col + d) % 8 for d in range(1, 8)]
-    for other in others:
-        pl.semaphore_signal(barrier, inc=1, device_id=(front, row, other), device_id_type=MESH)
-    pl.semaphore_wait(barrier, 7)
-    copies = [
-        pltpu.make_async_remote_copy(
-            src_ref=partial.at[other], dst_ref=arrived.at[d], send_sem=ssem.at[d], recv_sem=rsem.at[d],
-            device_id=(front, row, other), device_id_type=MESH,
-        )
-        for d, other in enumerate(others)
-    ]
-    for copy in copies:
-        copy.start()
-    total = partial[col].astype(F32)
-    for d, copy in enumerate(copies):
-        copy.wait()
-        total = total + arrived[d].astype(F32)
-    out[...] = total
-
-
-def product_sum(partial):
-    vmem = pl.BlockSpec(memory_space=pltpu.VMEM)
-    _, rows, wide = partial.shape
-    return pl.pallas_call(
-        product_kernel,
-        out_shape=jax.ShapeDtypeStruct((rows, wide), F32),
-        in_specs=[vmem],
-        out_specs=vmem,
-        scratch_shapes=[
-            pltpu.VMEM((7, rows, wide), BF16),
-            pltpu.SemaphoreType.DMA((7,)),
-            pltpu.SemaphoreType.DMA((7,)),
-        ],
-        compiler_params=pltpu.CompilerParams(collective_id=2, has_side_effects=True),
-        name="product_sum",
-    )(partial)
+    )(tables, own, theirs, contrib.reshape(16, TILE, 1024), init, vectors)
 
 
 def shards(pivot_block, border, contrib, inverses, row_tiles, col_tiles, owner, schur_init, block):
     tables, own, theirs = eliminate(row_tiles, col_tiles, owner, pivot_block, border, inverses)
-    arrived = exchanged_update(tables, own, theirs, contrib)
-    schur, partial = assemble(tables, arrived, schur_init, block)
-    return schur, product_sum(partial.reshape(8, 80, 512))
+    return exchanged_update(tables, own, theirs, contrib, schur_init, block)
 
 
 def solution(mesh):

time: 181 us -> 144 us (0.80)
  Pallas kernels: 177 us -> 136 us
  local copies, waits for them, and re-layouts: 1.59 us -> 4.55 us
    pallas_call x3 -> x1, Pallas kernels: 152 us -> 111 us  [exchanged_update(): pl.pallas_call(exchange_kernel, out_shape=(jax.ShapeDtypeStruct((rows, co...]
    unnamed x1 -> x4, local copies, waits for them, and re-layouts: 1.59 us -> 4.55 us
where the time goes in v3:
time: 144 us; the launch traced here: 141 us
  Pallas kernels  136 us (94%)
  local copies, waits for them, and re-layouts  4.55 us (3%)
    pallas_call x1, Pallas kernels, exchanged_update(): pl.pallas_call(exchange_kernel, out_shape=(jax.ShapeDtypeStruct((rows, co...  111 us
    pallas_call x1, Pallas kernels, eliminate(): pl.pallas_call(eliminate_kernel, out_shape=(jax.ShapeDtypeStruct((8, TILE...  24.8 us
    unnamed x4, local copies, waits for them, and re-layouts  4.55 us

profile of v3, /device:TPU:13, one launch (start us, length us, event | category | flops | bytes accessed | tf_op | source)
XLA Modules:
  0.0 140.9 jit_solution(2129713327644777839)
XLA Ops:
  0.6 24.8 %eliminate.1 = (s32[8,128]{1,0:T(8,128)}, bf16[16,128,1024]{2,1,0:T(8,128)(2,1)}, bf16[8,128,1024]{2,1,0:T(8,128)(2,1)}) custom-call(s32[4,64]{1,0:T(4,128)} %row_tiles.1, s32[4,64]{1,0:T(4,128)} %col_tiles.1, s32[1,80]{1,0:T(1,128)} %bitcast.5, bf16[1,1024,1024]{2,1,0:T(8,128)(2,1)} %pivot.1, bf16[16,128,1024]{2,1,0:T(8,128)(2,1)} %bitcast.3, ...), custom_call_target="tpu_custom_call" | custom-call | tf_op jit(solution)/shard_map/eliminate/pallas_call | solution.py:273
  25.5 110.8 %exchanged_update.1 = (f32[640,1280]{1,0:T(8,128)}, f32[80,512]{1,0:T(8,128)}) custom-call(s32[8,128]{1,0:T(8,128)} %get-tuple-element.5.tab, bf16[16,128,1024]{2,1,0:T(8,128)(2,1)} %get-tuple-element.6.own, bf16[8,128,1024]{2,1,0:T(8,128)(2,1)} %get-tuple-element.7.theirs, bf16[16,128,1024]{2,1,0:T(8,128)(2,1)} %bitcast.4, bf16[640,1280]{1,0:T(8,128)(2,1)} %init.1, ...), custom_call_target="tpu_custom_call" | custom-call | tf_op jit(solution)/shard_map/exchanged_update/pallas_call | solution.py:535
  136.3 0.0 copy-start
  136.3 3.9 %copy.13 = f32[640,1280]{1,0:T(8,128)} copy(f32[640,1280]{1,0:T(8,128)} %get-tuple-element.10) | data formatting | bytes 6553600
  140.2 0.0 copy-done
  140.2 0.7 copy.14
Async XLA Ops:
  136.3 3.9 %copy-start = (f32[80,512]{1,0:T(8,128)S(1)}, f32[80,512]{1,0:T(8,128)}, u32[]{:S(2)}) copy-start(f32[80,512]{1,0:T(8,128)} %get-tuple-element.11) | copy-start | bytes 491524

commit v4 on v3

--- a/solution.py
+++ b/solution.py
@@ -11,6 +11,10 @@
 MESH = pl.DeviceIdType.MESH
 F32 = jnp.float32
 BF16 = jnp.bfloat16
+
+
+def within(index, last):
+    return jnp.minimum(jnp.maximum(index, 0), last)
 
 
 def nt(a, b):
@@ -96,7 +100,9 @@
     t4 = table((g_c == front * 4 + row) & (f_c * 5 + a_c == q), mr + 1.0)
     t5 = table((h_c == col) & (f_c * 10 + b_c == q), mc + 1.0)
     zero = jnp.zeros_like(t0)
-    return jnp.concatenate([t0, t1, t2, t3, t4, t5, t6, zero], axis=0).astype(jnp.int32)
+    tops = (15.0, 7.0, 24.0, 7.0, 4.0, 8.0, 3.0, 0.0)
+    tables = [jnp.minimum(t, top) for t, top in zip((t0, t1, t2, t3, t4, t5, t6, zero), tops)]
+    return jnp.concatenate(tables, axis=0).astype(jnp.int32)
 
 
 def both_ways(ids):
@@ -138,56 +144,97 @@
     return parts
 
 
-def eliminate_kernel(
-    row_tiles, col_tiles, owner, pivot, border, inverse_set, tab, own_out, theirs_out,
-    rows_v, theirs, lower, lsem, osem, ssem, rsem,
+PARTS = 8
+
+
+ORDER1 = 11
+ORDER2 = 37
+
+
+def peer_of(front, z, core, x, u):
+    dk, dx, dz, dy = u & 1, (u >> 1) & 3, (u >> 3) & 3, u >> 5
+    f2, z2, k2, x2 = (front + dy) & 3, (z + dz) & 3, core ^ dk, (x + dx) & 3
+    return f2, ((z2 & 1) << 1) + k2, (x2 << 1) + (z2 >> 1)
+
+
+GROUP = 8
+UNIT = 16
+
+
+def front_kernel(
+    row_tiles, col_tiles, owner, pivot, border, contrib, inverse_set, init, vectors, schur, product,
+    tab_v, tab, rows_v, theirs, theirs_e, theirs_p, lower, contrib_v, left, packed, ordered, init_v, vectors_v, schur_v,
+    rounded, partial, sums, bsend, brecv, lsem, s1, r1, s2, r2, osem, s3, r3, *buffers,
 ):
+    spread, landed = buffers[:PARTS], buffers[PARTS:]
+    size = TILE // PARTS
+    units = size // UNIT
     front, z_lo, core, x, z_hi = position()
     z = z_hi * 2 + z_lo
-    up, down = (z + 1) % 4, (z + 3) % 4
+    row, col = lax.axis_index("row"), lax.axis_index("col")
+    here = row * 8 + col
+    everywhere = front * 32 + here
+    up, down = (z + 1) & 3, (z + 3) & 3
     on_source_chip = z_lo == x // 2
     is_source = on_source_chip & (core == x % 2)
     sibling = device(front, z, 1 - core, x)
     barrier = pltpu.get_barrier_semaphore()
-    for peer in (sibling, *(device(front, zz, k, x) for zz in (up, down) for k in (0, 1))):
-        pl.semaphore_signal(barrier, inc=1, device_id=peer, device_id_type=MESH)
+
+    def greet(u, _):
+        pl.semaphore_signal(barrier, inc=1, device_id=peer_of(front, z, core, x, u), device_id_type=MESH)
+        return 0
+
+    lax.fori_loop(1, 128, greet, 0)
     load_lower = pltpu.make_async_copy(pivot.at[0], lower, lsem.at[0])
     load_rows = pltpu.make_async_copy(border, rows_v, lsem.at[1])
+    load_init = pltpu.make_async_copy(init, init_v, lsem.at[2])
+    load_vectors = pltpu.make_async_copy(vectors, vectors_v, lsem.at[3])
+    load_contrib = [
+        pltpu.make_async_copy(
+            contrib.at[:, :, j * TILE : (j + 1) * TILE], contrib_v.at[j], lsem.at[4 + j]
+        )
+        for j in range(8)
+    ]
     load_lower.start()
     load_rows.start()
-    pl.semaphore_wait(barrier, 5)
-
-    def push(src, quarter, sem, peer):
+    pl.semaphore_wait(barrier, 127)
+
+    def push(src, tile, sem, peer):
         return pltpu.make_async_remote_copy(
-            src_ref=src, dst_ref=theirs.at[pl.ds(2 * quarter, 2)], send_sem=ssem.at[sem],
-            recv_sem=rsem.at[quarter], device_id=peer, device_id_type=MESH,
-        )
-
-    def quarter_of(half, q):
-        return border.at[pl.ds(half * 8 + q * 2, 2)]
+            src_ref=src, dst_ref=theirs.at[tile], send_sem=bsend.at[sem], recv_sem=brecv.at[tile],
+            device_id=peer, device_id_type=MESH,
+        )
 
     def source_sends():
         sends = []
-        for q in (0, 1):
-            sends.append(push(quarter_of(up // 2, q), q, q, device(front, up, q, x)))
-            sends.append(push(quarter_of(down // 2, 2 + q), 2 + q, 2 + q, device(front, down, q, x)))
-        for q in range(4):
-            sends.append(push(quarter_of(z_hi, q), q, 4 + q, sibling))
+        for tile in (0, 2, 1, 3, 4, 6, 5, 7):
+            to = down if tile & 2 else up
+            sends.append(push(border.at[(to >> 1) * 8 + tile], tile, tile, device(front, to, tile & 1, x)))
+        for tile in range(8):
+            sends.append(push(border.at[z_hi * 8 + tile], tile, 8 + tile, sibling))
         return sends
 
-    def own_quarters():
+    def own_tiles(first, last):
         return [
-            pltpu.make_async_copy(quarter_of(z_hi, q), theirs.at[pl.ds(2 * q, 2)], lsem.at[2 + q])
-            for q in range(4)
+            pltpu.make_async_copy(border.at[z_hi * 8 + t], theirs.at[t], lsem.at[12 + t]) for t in range(first, last)
         ]
 
     @pl.when(is_source)
     def _():
         for copy in source_sends():
             copy.start()
-        for copy in own_quarters():
+        for copy in own_tiles(0, 8):
             copy.start()
 
+    for copy in load_contrib:
+        copy.start()
+    load_init.start()
+    load_vectors.start()
+    rows_c, rows_r = both_ways(row_tiles[...])
+    cols_c, cols_r = both_ways(col_tiles[...])
+    tab_v[...] = routing(
+        rows_c, rows_r, cols_c, cols_r, owner[...], turned(owner[...].astype(F32)), front, row, col
+    )
     load_lower.wait()
     for k in range(3):
         low = (k + 1) * 256
@@ -201,167 +248,59 @@
         ).astype(BF16)
     load_rows.wait()
 
-    def block_of(buffer, target, base):
+    def block_of(source, target):
         def step(i, _):
             rows = pl.ds(i * 4, 4)
-            parts = eliminate_rows(buffer[rows].reshape(512, 1024), lower, inverse_set.at[0])
+            parts = eliminate_rows(source[rows].reshape(512, 1024), lower, inverse_set.at[0])
             for k in range(4):
-                buffer[rows, :, k * 256 : (k + 1) * 256] = parts[k].reshape(4, TILE, 256)
-            pltpu.make_async_copy(buffer.at[rows], target.at[rows], osem.at[base + i]).start()
+                target[rows, :, k * 256 : (k + 1) * 256] = parts[k].reshape(4, TILE, 256)
             return 0
 
         return step
 
-    lax.fori_loop(0, 4, block_of(rows_v, own_out, 0), 0)
-    rows_c, rows_r = both_ways(row_tiles[...])
-    cols_c, cols_r = both_ways(col_tiles[...])
-    tab[...] = routing(
-        rows_c, rows_r, cols_c, cols_r, owner[...], turned(owner[...].astype(F32)),
-        front, lax.axis_index("row"), lax.axis_index("col"),
-    )
-
-    def wait_quarter(q):
-        push(theirs.at[pl.ds(2 * q, 2)], q, 0, sibling).wait_recv()
-
-    def forwards():
-        return [
-            push(theirs.at[pl.ds(2 * q, 2)], q, i, sibling) for i, q in enumerate((core, 2 + core))
-        ]
-
-    @pl.when(is_source)
-    def _():
-        for copy in own_quarters():
-            copy.wait()
-
-    @pl.when(jnp.logical_not(on_source_chip))
-    def _():
-        first, second = forwards()
-        wait_quarter(core)
-        first.start()
-        wait_quarter(2 + core)
-        second.start()
-        wait_quarter(1 - core)
-        wait_quarter(3 - core)
-
-    @pl.when(on_source_chip & jnp.logical_not(is_source))
-    def _():
-        for q in range(4):
-            wait_quarter(q)
-
-    @pl.when(is_source)
-    def _():
-        for copy in source_sends():
-            copy.wait_send()
-
-    @pl.when(jnp.logical_not(on_source_chip))
-    def _():
-        for copy in forwards():
-            copy.wait_send()
-
-    lax.fori_loop(0, 2, block_of(theirs, theirs_out, 4), 0)
-    for i in range(4):
-        rows = pl.ds(i * 4, 4)
-        pltpu.make_async_copy(rows_v.at[rows], own_out.at[rows], osem.at[i]).wait()
+    lax.fori_loop(0, 4, block_of(rows_v, rows_v), 0)
+    table_copy = pltpu.make_async_copy(tab_v, tab, lsem.at[20])
+    table_copy.start()
+
+    def wait_tile(t):
+        push(theirs.at[t], t, 0, sibling).wait_recv()
+
+    def forward(t):
+        return push(theirs.at[t], t, t >> 1, sibling)
+
     for i in range(2):
-        rows = pl.ds(i * 4, 4)
-        pltpu.make_async_copy(theirs.at[rows], theirs_out.at[rows], osem.at[4 + i]).wait()
-
-
-def eliminate(row_tiles, col_tiles, owner, pivot, border, inverse_set):
-    vmem = pl.BlockSpec(memory_space=pltpu.VMEM)
-    hbm = pl.BlockSpec(memory_space=pl.ANY)
-    return pl.pallas_call(
-        eliminate_kernel,
-        out_shape=(
-            jax.ShapeDtypeStruct((8, TILE), jnp.int32),
-            jax.ShapeDtypeStruct((16, TILE, 1024), BF16),
-            jax.ShapeDtypeStruct((8, TILE, 1024), BF16),
-        ),
-        in_specs=[vmem, vmem, vmem, hbm, hbm, vmem],
-        out_specs=(vmem, hbm, hbm),
-        scratch_shapes=[
-            pltpu.VMEM((16, TILE, 1024), BF16),
-            pltpu.VMEM((8, TILE, 1024), BF16),
-            pltpu.VMEM((1024, 1024), BF16),
-            pltpu.SemaphoreType.DMA((6,)),
-            pltpu.SemaphoreType.DMA((6,)),
-            pltpu.SemaphoreType.DMA((8,)),
-            pltpu.SemaphoreType.DMA((4,)),
-        ],
-        compiler_params=pltpu.CompilerParams(
-            collective_id=0, has_side_effects=True, vmem_limit_bytes=60 << 20
-        ),
-        name="eliminate",
-    )(
-        row_tiles, col_tiles, owner.reshape(1, owner.size), pivot,
-        border.reshape(16, TILE, 1024), inverse_set,
-    )
-
-
-PARTS = 8
-
-
-ORDER1 = 11
-ORDER2 = 37
-
-
-def peer_of(front, z, core, x, u):
-    dk, dx, dz, dy = u & 1, (u >> 1) & 3, (u >> 3) & 3, u >> 5
-    f2, z2, k2, x2 = (front + dy) & 3, (z + dz) & 3, core ^ dk, (x + dx) & 3
-    return f2, ((z2 & 1) << 1) + k2, (x2 << 1) + (z2 >> 1)
-
-
-GROUP = 8
-UNIT = 16
-
-
-def exchange_kernel(
-    tab, own, theirs, contrib, init, vectors, schur, product,
-    own_v, theirs_v, theirs_p, contrib_v, left, packed, ordered, init_v, vectors_v, schur_v, rounded, partial, sums,
-    lsem, s1, r1, s2, r2, osem, s3, r3, *buffers,
-):
-    spread, landed = buffers[:PARTS], buffers[PARTS:]
-    size = TILE // PARTS
-    units = size // UNIT
-    front, z_lo, core, x, z_hi = position()
-    z = z_hi * 2 + z_lo
-    row, col = lax.axis_index("row"), lax.axis_index("col")
-    here = row * 8 + col
-    everywhere = front * 32 + here
-    barrier = pltpu.get_barrier_semaphore()
-
-    def greet(u, _):
-        pl.semaphore_signal(barrier, inc=1, device_id=peer_of(front, z, core, x, u), device_id_type=MESH)
-        return 0
-
-    lax.fori_loop(1, 128, greet, 0)
-    load_theirs = pltpu.make_async_copy(theirs, theirs_v, lsem.at[0])
-    load_own = pltpu.make_async_copy(own, own_v, lsem.at[1])
-    load_contrib = [
-        pltpu.make_async_copy(
-            contrib.at[:, :, j * TILE : (j + 1) * TILE], contrib_v.at[j], lsem.at[4 + j]
-        )
-        for j in range(8)
-    ]
-    load_init = pltpu.make_async_copy(init, init_v, lsem.at[2])
-    load_vectors = pltpu.make_async_copy(vectors, vectors_v, lsem.at[3])
-    load_theirs.start()
-    load_own.start()
-    for copy in load_contrib:
-        copy.start()
-    load_init.start()
-    load_vectors.start()
-    load_theirs.wait()
+        base = 4 * i
+
+        @pl.when(is_source)
+        def _():
+            for copy in own_tiles(base, base + 4):
+                copy.wait()
+
+        @pl.when(jnp.logical_not(on_source_chip))
+        def _():
+            for t in (base + core, base + 2 + core):
+                wait_tile(t)
+                forward(t).start()
+            for t in (base + 1 - core, base + 3 - core):
+                wait_tile(t)
+
+        @pl.when(on_source_chip & jnp.logical_not(is_source))
+        def _():
+            for t in range(base, base + 4):
+                wait_tile(t)
+
+        block_of(theirs, theirs_e)(i, 0)
+
+    table_copy.wait()
     for m in range(8):
-        theirs_p[m] = theirs_v[tab[1, m]]
-    load_own.wait()
+        theirs_p[m] = theirs_e[within(tab[1, m], 7)]
     for copy in load_contrib:
         copy.wait()
 
     def update(s):
         rows = slice(s * size, (s + 1) * size)
         for q in range(16):
-            left[q] = own_v[tab[0, q], rows]
+            left[q] = rows_v[within(tab[0, q], 15), rows]
 
         def two_cols(n, _):
             product = nt(
@@ -369,7 +308,7 @@
             )
             for t in range(2):
                 for q in range(16):
-                    tile = contrib_v[tab[1, 2 * n + t], tab[0, q], rows].astype(F32)
+                    tile = contrib_v[within(tab[1, 2 * n + t], 7), within(tab[0, q], 15), rows].astype(F32)
                     part = product[q * size : (q + 1) * size, t * TILE : (t + 1) * TILE]
                     packed[s, (q // 4) * 8 + 2 * n + t, q % 4] = (tile - part).astype(BF16)
             return 0
@@ -410,7 +349,7 @@
         def fill(t):
             f2, row2, col2 = second_peer(t)
             g = f2 * 4 + row2
-            ordered[s, t] = spread[s][tab[2, g] + tab[3, col2], tab[6, g]]
+            ordered[s, t] = spread[s][within(tab[2, g] + tab[3, col2], 31), within(tab[6, g], 3)]
 
         for t in range(GROUP):
             fill(t)
@@ -449,7 +388,7 @@
                 for f in range(4):
                     m, k = tab[4, f * 5 + a], tab[5, f * 10 + b]
                     at = f * 32 + jnp.maximum(m - 1, 0) * 8 + jnp.maximum(k - 1, 0)
-                    total = total + jnp.where((m > 0) & (k > 0), landed[s][at].astype(F32), 0.0)
+                    total = total + jnp.where((m > 0) & (k > 0), landed[s][within(at, 127)].astype(F32), 0.0)
                 schur_v[rows, cols] = total
                 rounded[pl.ds(pl.multiple_of(a * size, size), size), cols] = total.astype(BF16)
             return 0
@@ -501,8 +440,6 @@
 
     for s in range(PARTS):
         update(s)
-        if s == 0:
-            pl.semaphore_wait(barrier, 127)
         first_send(s)
     for s in range(PARTS):
         first_all(s).wait_recv()
@@ -526,24 +463,39 @@
         for a in range(5):
             write(a, s).wait()
 
-
-def exchanged_update(tables, own, theirs, contrib, init, vectors):
+    @pl.when(is_source)
+    def _():
+        for copy in source_sends():
+            copy.wait_send()
+
+    @pl.when(jnp.logical_not(on_source_chip))
+    def _():
+        for i in range(4):
+            forward(2 * i + core).wait_send()
+
+
+def fronts(row_tiles, col_tiles, owner, pivot, border, contrib, inverse_set, init, vectors):
     hbm = pl.BlockSpec(memory_space=pl.ANY)
+    vmem = pl.BlockSpec(memory_space=pltpu.VMEM)
     size = TILE // PARTS
     rows, cols = init.shape
     wide = vectors.shape[1]
     return pl.pallas_call(
-        exchange_kernel,
+        front_kernel,
         out_shape=(
             jax.ShapeDtypeStruct((rows, cols), F32),
             jax.ShapeDtypeStruct((rows // 8, wide), F32),
         ),
-        in_specs=[pl.BlockSpec(memory_space=pltpu.SMEM), hbm, hbm, hbm, hbm, hbm],
-        out_specs=(hbm, pl.BlockSpec(memory_space=pltpu.VMEM)),
+        in_specs=[vmem, vmem, vmem, hbm, hbm, hbm, vmem, hbm, hbm],
+        out_specs=(hbm, vmem),
         scratch_shapes=[
+            pltpu.VMEM((8, TILE), jnp.int32),
+            pltpu.SMEM((8, TILE), jnp.int32),
             pltpu.VMEM((16, TILE, 1024), BF16),
             pltpu.VMEM((8, TILE, 1024), BF16),
             pltpu.VMEM((8, TILE, 1024), BF16),
+            pltpu.VMEM((8, TILE, 1024), BF16),
+            pltpu.VMEM((1024, 1024), BF16),
             pltpu.VMEM((8, 16, TILE, TILE), BF16),
             pltpu.VMEM((16, size, 1024), BF16),
             pltpu.VMEM((PARTS, 32, 4, size, TILE), BF16),
@@ -554,7 +506,9 @@
             pltpu.VMEM((5 * size, cols), BF16),
             pltpu.VMEM((PARTS, 5, size // UNIT, UNIT, wide), BF16),
             pltpu.VMEM((8, 5, UNIT, wide), BF16),
-            pltpu.SemaphoreType.DMA((12,)),
+            pltpu.SemaphoreType.DMA((16,)),
+            pltpu.SemaphoreType.DMA((8,)),
+            pltpu.SemaphoreType.DMA((21,)),
             *[pltpu.SemaphoreType.DMA((PARTS,))] * 4,
             pltpu.SemaphoreType.DMA((PARTS, 5)),
             pltpu.SemaphoreType.DMA,
@@ -563,15 +517,19 @@
             *[pltpu.VMEM((128, size, TILE), BF16)] * PARTS,
         ],
         compiler_params=pltpu.CompilerParams(
-            collective_id=1, has_side_effects=True, vmem_limit_bytes=60 << 20
+            collective_id=0, has_side_effects=True, vmem_limit_bytes=60 << 20
         ),
-        name="exchanged_update",
-    )(tables, own, theirs, contrib.reshape(16, TILE, 1024), init, vectors)
+        name="fronts",
+    )(
+        row_tiles, col_tiles, owner.reshape(1, owner.size), pivot, border.reshape(16, TILE, 1024),
+        contrib.reshape(16, TILE, 1024), inverse_set, init, vectors,
+    )
 
 
 def shards(pivot_block, border, contrib, inverses, row_tiles, col_tiles, owner, schur_init, block):
-    tables, own, theirs = eliminate(row_tiles, col_tiles, owner, pivot_block, border, inverses)
-    return exchanged_update(tables, own, theirs, contrib, schur_init, block)
+    return fronts(
+        row_tiles, col_tiles, owner, pivot_block, border, contrib, inverses, schur_init, block
+    )
 
 
 def solution(mesh):

time: 144 us -> 141 us (0.979); the launches traced: 141 us -> 141 us
    pallas_call x2 -> x1, Pallas kernels: 136 us -> 136 us  [fronts(): pl.pallas_call(front_kernel, out_shape=(jax.ShapeDtypeStruct((rows, cols)...]
where the time goes in v4:
time: 141 us
  Pallas kernels  136 us (96%)
  local copies, waits for them, and re-layouts  4.55 us (3%)
    pallas_call x1, Pallas kernels, fronts(): pl.pallas_call(front_kernel, out_shape=(jax.ShapeDtypeStruct((rows, cols)...  136 us
    unnamed x4, local copies, waits for them, and re-layouts  4.55 us

profile of v4, /device:TPU:13, one launch (start us, length us, event | category | flops | bytes accessed | tf_op | source)
XLA Modules:
  0.0 140.9 jit_solution(12732445881139683368)
XLA Ops:
  0.6 135.7 %fronts.1 = (f32[640,1280]{1,0:T(8,128)}, f32[80,512]{1,0:T(8,128)}) custom-call(s32[4,64]{1,0:T(4,128)} %row_tiles.1, s32[4,64]{1,0:T(4,128)} %col_tiles.1, s32[1,80]{1,0:T(1,128)} %bitcast.5, bf16[1,1024,1024]{2,1,0:T(8,128)(2,1)} %pivot.1, bf16[16,128,1024]{2,1,0:T(8,128)(2,1)} %bitcast.3, bf16[16,128,1024]{2,1,0:T(8,128)(2,1)} %bitcast.4, ...), custom_call_target="tpu_custom_call" | custom-call | tf_op jit(solution)/shard_map/fronts/pallas_call | solution.py:483
  136.3 0.0 copy-start
  136.4 3.9 %copy.13 = f32[640,1280]{1,0:T(8,128)} copy(f32[640,1280]{1,0:T(8,128)} %get-tuple-element.4) | data formatting | bytes 6553600
  140.2 0.0 copy-done
  140.2 0.7 copy.14
Async XLA Ops:
  136.3 3.9 %copy-start = (f32[80,512]{1,0:T(8,128)S(1)}, f32[80,512]{1,0:T(8,128)}, u32[]{:S(2)}) copy-start(f32[80,512]{1,0:T(8,128)} %get-tuple-element.5) | copy-start | bytes 491524

commit v5 on v4

--- a/solution.py
+++ b/solution.py
@@ -53,6 +53,9 @@
     return color_c
 
 
+TABLE_ROWS = ((16, 15), (8, 7), (16, 24), (8, 7), (20, 4), (40, 8), (16, 3))
+
+
 def div(x, by):
     return jnp.floor((x + 0.5) * (1.0 / by))
 
@@ -163,7 +166,7 @@
 
 def front_kernel(
     row_tiles, col_tiles, owner, pivot, border, contrib, inverse_set, init, vectors, schur, product,
-    tab_v, tab, rows_v, theirs, theirs_e, theirs_p, lower, contrib_v, left, packed, ordered, init_v, vectors_v, schur_v,
+    tab_v, tab_raw, tab, rows_v, theirs, theirs_e, theirs_p, lower, contrib_v, left, packed, ordered, init_v, vectors_v, schur_v,
     rounded, partial, sums, bsend, brecv, lsem, s1, r1, s2, r2, osem, s3, r3, *buffers,
 ):
     spread, landed = buffers[:PARTS], buffers[PARTS:]
@@ -259,7 +262,7 @@
         return step
 
     lax.fori_loop(0, 4, block_of(rows_v, rows_v), 0)
-    table_copy = pltpu.make_async_copy(tab_v, tab, lsem.at[20])
+    table_copy = pltpu.make_async_copy(tab_v, tab_raw, lsem.at[20])
     table_copy.start()
 
     def wait_tile(t):
@@ -292,15 +295,18 @@
         block_of(theirs, theirs_e)(i, 0)
 
     table_copy.wait()
+    for r, (count, last) in enumerate(TABLE_ROWS):
+        for at in range(count):
+            tab[r, at] = within(tab_raw[r, at], last)
     for m in range(8):
-        theirs_p[m] = theirs_e[within(tab[1, m], 7)]
+        theirs_p[m] = theirs_e[tab[1, m]]
     for copy in load_contrib:
         copy.wait()
 
     def update(s):
         rows = slice(s * size, (s + 1) * size)
         for q in range(16):
-            left[q] = rows_v[within(tab[0, q], 15), rows]
+            left[q] = rows_v[tab[0, q], rows]
 
         def two_cols(n, _):
             product = nt(
@@ -308,7 +314,7 @@
             )
             for t in range(2):
                 for q in range(16):
-                    tile = contrib_v[within(tab[1, 2 * n + t], 7), within(tab[0, q], 15), rows].astype(F32)
+                    tile = contrib_v[tab[1, 2 * n + t], tab[0, q], rows].astype(F32)
                     part = product[q * size : (q + 1) * size, t * TILE : (t + 1) * TILE]
                     packed[s, (q // 4) * 8 + 2 * n + t, q % 4] = (tile - part).astype(BF16)
             return 0
@@ -349,7 +355,7 @@
         def fill(t):
             f2, row2, col2 = second_peer(t)
             g = f2 * 4 + row2
-            ordered[s, t] = spread[s][within(tab[2, g] + tab[3, col2], 31), within(tab[6, g], 3)]
+            ordered[s, t] = spread[s][tab[2, g] + tab[3, col2], tab[6, g]]
 
         for t in range(GROUP):
             fill(t)
@@ -388,7 +394,7 @@
                 for f in range(4):
                     m, k = tab[4, f * 5 + a], tab[5, f * 10 + b]
                     at = f * 32 + jnp.maximum(m - 1, 0) * 8 + jnp.maximum(k - 1, 0)
-                    total = total + jnp.where((m > 0) & (k > 0), landed[s][within(at, 127)].astype(F32), 0.0)
+                    total = total + jnp.where((m > 0) & (k > 0), landed[s][at].astype(F32), 0.0)
                 schur_v[rows, cols] = total
                 rounded[pl.ds(pl.multiple_of(a * size, size), size), cols] = total.astype(BF16)
             return 0
@@ -490,6 +496,7 @@
         out_specs=(hbm, vmem),
         scratch_shapes=[
             pltpu.VMEM((8, TILE), jnp.int32),
+            pltpu.SMEM((8, TILE), jnp.int32),
             pltpu.SMEM((8, TILE), jnp.int32),
             pltpu.VMEM((16, TILE, 1024), BF16),
             pltpu.VMEM((8, TILE, 1024), BF16),

time: 141 us -> 139 us (0.986)
  Pallas kernels: 136 us -> 134 us
    pallas_call x1, Pallas kernels: 136 us -> 134 us  [fronts(): pl.pallas_call(front_kernel, out_shape=(jax.ShapeDtypeStruct((rows, cols)...]
where the time goes in v5:
time: 139 us
  Pallas kernels  134 us (96%)
  local copies, waits for them, and re-layouts  4.55 us (3%)
    pallas_call x1, Pallas kernels, fronts(): pl.pallas_call(front_kernel, out_shape=(jax.ShapeDtypeStruct((rows, cols)...  134 us
    unnamed x4, local copies, waits for them, and re-layouts  4.55 us

profile of v5, /device:TPU:13, one launch (start us, length us, event | category | flops | bytes accessed | tf_op | source)
XLA Modules:
  0.0 139.1 jit_solution(10953300050254601442)
XLA Ops:
  0.6 133.9 %fronts.1 = (f32[640,1280]{1,0:T(8,128)}, f32[80,512]{1,0:T(8,128)}) custom-call(s32[4,64]{1,0:T(4,128)} %row_tiles.1, s32[4,64]{1,0:T(4,128)} %col_tiles.1, s32[1,80]{1,0:T(1,128)} %bitcast.5, bf16[1,1024,1024]{2,1,0:T(8,128)(2,1)} %pivot.1, bf16[16,128,1024]{2,1,0:T(8,128)(2,1)} %bitcast.3, bf16[16,128,1024]{2,1,0:T(8,128)(2,1)} %bitcast.4, ...), custom_call_target="tpu_custom_call" | custom-call | tf_op jit(solution)/shard_map/fronts/pallas_call | solution.py:489
  134.6 0.0 copy-start
  134.6 3.9 %copy.13 = f32[640,1280]{1,0:T(8,128)} copy(f32[640,1280]{1,0:T(8,128)} %get-tuple-element.4) | data formatting | bytes 6553600
  138.5 0.0 copy-done
  138.5 0.7 copy.14
Async XLA Ops:
  134.6 3.9 %copy-start = (f32[80,512]{1,0:T(8,128)S(1)}, f32[80,512]{1,0:T(8,128)}, u32[]{:S(2)}) copy-start(f32[80,512]{1,0:T(8,128)} %get-tuple-element.5) | copy-start | bytes 491524

commit v6 on v5

--- a/solution.py
+++ b/solution.py
@@ -271,28 +271,43 @@
     def forward(t):
         return push(theirs.at[t], t, t >> 1, sibling)
 
-    for i in range(2):
-        base = 4 * i
+    for tiles in ((0, 2, 1, 3), (4, 6), (5, 7)):
 
         @pl.when(is_source)
         def _():
-            for copy in own_tiles(base, base + 4):
-                copy.wait()
+            for t in tiles:
+                for copy in own_tiles(t, t + 1):
+                    copy.wait()
 
         @pl.when(jnp.logical_not(on_source_chip))
         def _():
-            for t in (base + core, base + 2 + core):
-                wait_tile(t)
-                forward(t).start()
-            for t in (base + 1 - core, base + 3 - core):
-                wait_tile(t)
+            for parity in (0, 1):
+                mine = [t for t in tiles if t % 2 == parity]
+
+                @pl.when(core == parity)
+                def _():
+                    for t in mine:
+                        wait_tile(t)
+                        forward(t).start()
+
+            for parity in (0, 1):
+                other = [t for t in tiles if t % 2 == parity]
+
+                @pl.when(core != parity)
+                def _():
+                    for t in other:
+                        wait_tile(t)
 
         @pl.when(on_source_chip & jnp.logical_not(is_source))
         def _():
-            for t in range(base, base + 4):
+            for t in tiles:
                 wait_tile(t)
 
-        block_of(theirs, theirs_e)(i, 0)
+        joined = jnp.concatenate([theirs[t] for t in tiles], axis=0)
+        parts = eliminate_rows(joined, lower, inverse_set.at[0])
+        for i, t in enumerate(tiles):
+            for k in range(4):
+                theirs_e[t, :, k * 256 : (k + 1) * 256] = parts[k][i * TILE : (i + 1) * TILE]
 
     table_copy.wait()
     for r, (count, last) in enumerate(TABLE_ROWS):

time: 139 us -> 142 us (1.022); the launches traced: 139 us -> 140 us
  no operation moved by 1% of the time
where the time goes in v6:
time: 142 us; the launch traced here: 140 us
  Pallas kernels  135 us (95%)
  local copies, waits for them, and re-layouts  4.55 us (3%)
    pallas_call x1, Pallas kernels, fronts(): pl.pallas_call(front_kernel, out_shape=(jax.ShapeDtypeStruct((rows, cols)...  135 us
    unnamed x4, local copies, waits for them, and re-layouts  4.55 us

profile of v6, /device:TPU:13, one launch (start us, length us, event | category | flops | bytes accessed | tf_op | source)
XLA Modules:
  0.0 140.0 jit_solution(6622003625919914393)
XLA Ops:
  0.6 134.8 %fronts.1 = (f32[640,1280]{1,0:T(8,128)}, f32[80,512]{1,0:T(8,128)}) custom-call(s32[4,64]{1,0:T(4,128)} %row_tiles.1, s32[4,64]{1,0:T(4,128)} %col_tiles.1, s32[1,80]{1,0:T(1,128)} %bitcast.5, bf16[1,1024,1024]{2,1,0:T(8,128)(2,1)} %pivot.1, bf16[16,128,1024]{2,1,0:T(8,128)(2,1)} %bitcast.3, bf16[16,128,1024]{2,1,0:T(8,128)(2,1)} %bitcast.4, ...), custom_call_target="tpu_custom_call" | custom-call | tf_op jit(solution)/shard_map/fronts/pallas_call | solution.py:504
  135.5 0.0 copy-start
  135.5 3.9 %copy.13 = f32[640,1280]{1,0:T(8,128)} copy(f32[640,1280]{1,0:T(8,128)} %get-tuple-element.4) | data formatting | bytes 6553600
  139.3 0.0 copy-done
  139.3 0.7 copy.14
Async XLA Ops:
  135.5 3.9 %copy-start = (f32[80,512]{1,0:T(8,128)S(1)}, f32[80,512]{1,0:T(8,128)}, u32[]{:S(2)}) copy-start(f32[80,512]{1,0:T(8,128)} %get-tuple-element.5) | copy-start | bytes 491524
